TPU v7x, 128 devices: a whole 4x4x4 slice. The times are simulated.
128 devices in a mesh: seq: 32 (over x, y, z_hi), dp: 4 (over z_lo, core).
Axes of the slice: x: 4, y: 4, z: 4 (z_hi: 2, z_lo: 2; z = z_hi * 2 + z_lo), core: 2. Of those that a mesh axis runs over, the one named last changes fastest.
Arguments:
- queries: bfloat16 [4, 12288, 2048], P('dp', 'seq'), may hold values from -40 to 40
- keys: bfloat16 [4, 12288, 2048], P('dp', 'seq'), may hold values from -40 to 40
- values: bfloat16 [4, 12288, 2048], P('dp', 'seq'), may hold values from -6 to 6
- out_grad: bfloat16 [4, 12288, 2048], P('dp', 'seq'), may hold values from -6 to 6
- proj_weight: bfloat16 [2048, 2048], P('dp'), may hold values from -0.125 to 0.125
- lengths: int32 [4], P('dp'), may hold values from 3072 to 12288
Outputs:
- query_grad: bfloat16 [4, 12288, 2048], P('dp', 'seq')
- key_grad: bfloat16 [4, 12288, 2048], P('dp', 'seq')
- value_grad: bfloat16 [4, 12288, 2048], P('dp', 'seq')
- weight_grad: float32 [2048, 2048], P('dp', 'seq')
All inputs are finite; a program needn't handle non-finite values.
Results may differ from a plain program's by a relative error of at most 0.019.
Values may be sent and summed in bfloat16 or wider, within the bound.
A program may use at most 192 MiB of HBM per device.

v0:
```python
import jax
import jax.numpy as jnp
from jax import lax
from jax.sharding import PartitionSpec as P

HEAD_DIM = 128
CYCLE = 2


def from_behind(block, axis, distance):
    devices = range(lax.axis_size(axis))
    route = [(i - distance, i) for i in devices if i - distance in devices]
    return lax.ppermute(block, axis, route)


def cut_along(shard, dim, count):
    before, after = (shard.shape[:dim], shard.shape[dim + 1 :])
    return jnp.moveaxis(shard.reshape(*before, count, -1, *after), dim, 0)


def sum_at_owner(shard, axis, dim):
    pieces = cut_along(shard, dim, lax.axis_size(axis))
    arrived = lax.all_to_all(pieces, axis, split_axis=0, concat_axis=0, tiled=True)
    return arrived.astype(jnp.float32).sum(axis=0)


def sent_and_summed(shard, axis, dim):
    count = lax.axis_size(axis)
    pieces = lax.all_to_all(cut_along(shard, dim, count), axis, 0, 0, tiled=True)
    return jnp.sum(pieces, axis=0)


def per_device(queries, keys, values, out_grad, proj_weight, lengths):
    scale = HEAD_DIM ** (-0.5)
    query_rows = queries[0]
    key_rows = keys[0]
    value_rows = values[0]
    grad_rows = out_grad[0]
    tokens = query_rows.shape[0]
    width = query_rows.shape[1]
    heads = width // HEAD_DIM
    position = lax.axis_index("seq")
    query_pos = position * tokens + jnp.arange(tokens, dtype=jnp.int32)
    live = (query_pos < lengths[0]).astype(jnp.bfloat16)
    grad_masked = grad_rows * live[:, None]
    everyone = lax.all_gather(grad_masked[None], "dp", axis=0, tiled=True)
    column_part = jnp.einsum(
        "btd,fd->btf", everyone, proj_weight, preferred_element_type=jnp.float32
    ).astype(jnp.bfloat16)
    out_bwd = lax.all_to_all(column_part, "dp", split_axis=0, concat_axis=2, tiled=True)[0]
    blocks = [(key_rows, value_rows)]
    for offset in range(1, CYCLE + 1):
        blocks.append(from_behind((key_rows, value_rows), "seq", offset))
    query_heads = query_rows.reshape(tokens, heads, HEAD_DIM)
    causal = jnp.arange(tokens)[:, None] >= jnp.arange(tokens)[None, :]
    score_list = []
    for offset in range(CYCLE + 1):
        key_heads = blocks[offset][0].reshape(tokens, heads, HEAD_DIM)
        scores = (
            jnp.einsum("thd,shd->hts", query_heads, key_heads, preferred_element_type=jnp.float32)
            * scale
        )
        if offset == 0:
            scores = jnp.where(causal[None], scores, -1e30)
        else:
            scores = jnp.where(position >= offset, scores, -1e30)
        score_list.append(scores)
    maximum = score_list[0].max(axis=2, keepdims=True)
    for scores in score_list[1:]:
        maximum = jnp.maximum(maximum, scores.max(axis=2, keepdims=True))
    total = jnp.zeros_like(maximum)
    for scores in score_list:
        total = total + jnp.sum(jnp.exp(scores - maximum), axis=2, keepdims=True)
    lse = maximum + jnp.log(total)
    prob_list = []
    attn_sum = jnp.zeros((tokens, heads, HEAD_DIM), jnp.float32)
    for offset in range(CYCLE + 1):
        probs = jnp.exp(score_list[offset] - lse)
        probs_b = probs.astype(jnp.bfloat16)
        prob_list.append((probs, probs_b))
        value_heads = blocks[offset][1].reshape(tokens, heads, HEAD_DIM)
        attn_sum = attn_sum + jnp.einsum(
            "hts,shd->thd", probs_b, value_heads, preferred_element_type=jnp.float32
        )
    attn_out = attn_sum.astype(jnp.bfloat16)
    out_heads = out_bwd.reshape(tokens, heads, HEAD_DIM)
    delta = jnp.sum(out_heads.astype(jnp.float32) * attn_out.astype(jnp.float32), axis=2)
    delta_rows = delta.T[:, :, None]
    query_accum = jnp.zeros((tokens, heads, HEAD_DIM), jnp.float32)
    key_accum = jnp.zeros((tokens, width), jnp.float32)
    value_accum = jnp.zeros((tokens, width), jnp.float32)
    for offset in range(CYCLE + 1):
        key_heads = blocks[offset][0].reshape(tokens, heads, HEAD_DIM)
        value_heads = blocks[offset][1].reshape(tokens, heads, HEAD_DIM)
        probs, probs_b = prob_list[offset]
        prob_grad = jnp.einsum(
            "thd,shd->hts", out_heads, value_heads, preferred_element_type=jnp.float32
        )
        score_grad = (probs * (prob_grad - delta_rows) * scale).astype(jnp.bfloat16)
        query_accum = query_accum + jnp.einsum(
            "hts,shd->thd", score_grad, key_heads, preferred_element_type=jnp.float32
        )
        key_term = (
            jnp.einsum("hts,thd->shd", score_grad, query_heads, preferred_element_type=jnp.float32)
            .astype(jnp.bfloat16)
            .reshape(tokens, width)
        )
        value_term = (
            jnp.einsum("hts,thd->shd", probs_b, out_heads, preferred_element_type=jnp.float32)
            .astype(jnp.bfloat16)
            .reshape(tokens, width)
        )
        if offset > 0:
            key_term, value_term = from_behind((key_term, value_term), "seq", -offset)
        key_accum = key_accum + key_term.astype(jnp.float32)
        value_accum = value_accum + value_term.astype(jnp.float32)
    attn_flat = attn_out.reshape(tokens, width)
    whole_term = lax.dot_general(
        attn_flat, grad_masked, (((0,), (0,)), ((), ())), preferred_element_type=jnp.float32
    )
    column_sums = sum_at_owner(whole_term.astype(jnp.bfloat16), "seq", 1)
    weight_grad = sent_and_summed(column_sums, "dp", 0)
    query_grad = query_accum.reshape(tokens, width).astype(jnp.bfloat16)
    return (
        query_grad[None],
        key_accum.astype(jnp.bfloat16)[None],
        value_accum.astype(jnp.bfloat16)[None],
        weight_grad,
    )


def solution(mesh):
    placed = (
        P("dp", "seq", None),
        P("dp", "seq", None),
        P("dp", "seq", None),
        P("dp", "seq", None),
        P("dp", None),
        P("dp"),
    )
    return jax.shard_map(
        per_device,
        mesh=mesh,
        in_specs=placed,
        out_specs=(
            P("dp", "seq", None),
            P("dp", "seq", None),
            P("dp", "seq", None),
            P("dp", "seq"),
        ),
        check_vma=False,
    )
```

profile of v0, /device:TPU:60, one launch (start us, length us, event | category | flops | bytes accessed | tf_op | source)
XLA Modules:
  0.0 480.3 jit_solution(17212700500421851630)
XLA Ops:
  33.2 7.4 %fusion.3 = (f32[16,384]{1,0:T(8,128)S(1)}, f32[16,384,384]{1,2,0:T(8,128)}) fusion(pred[384,384]{0,1:T(8,128)(4,1)S(1)} %iota_compare_fusion, bf16[384,16,128]{0,2,1:T(8,128)(2,1)} %bitcast.92, bf16[384,16,128]{0,2,1:T(8,128)(2,1)} %bitcast.104), kind=kOutput, calls=%fused_computation.17 | convolution fusion | flops 611051520 | bytes 12754944 | tf_op jit(solution)/shard_map/thd,shd->hts/dot_general | solution.py:60
  40.6 9.6 %collective-permute-done.3 = bf16[384,2048]{1,0:T(8,128)(2,1)} collective-permute-done((bf16[384,2048]{1,0:T(8,128)(2,1)}, bf16[384,2048]{1,0:T(8,128)(2,1)}, u32[]{:S(2)}, u32[]{:S(2)}) %collective-permute-start.3) | collective-permute-done | bytes 1572896 | tf_op jit(solution)/shard_map/ppermute | solution.py:13
  52.9 33.6 %collective-permute-done.2 = bf16[384,2048]{1,0:T(8,128)(2,1)} collective-permute-done((bf16[384,2048]{1,0:T(8,128)(2,1)}, bf16[384,2048]{1,0:T(8,128)(2,1)}, u32[]{:S(2)}, u32[]{:S(2)}) %collective-permute-start.2) | collective-permute-done | bytes 1572896 | tf_op jit(solution)/shard_map/ppermute | solution.py:13
  89.1 47.3 %collective-permute-done = bf16[384,2048]{0,1:T(8,128)(2,1)} collective-permute-done((bf16[384,2048]{0,1:T(8,128)(2,1)}, bf16[384,2048]{0,1:T(8,128)(2,1)}, u32[]{:S(2)}, u32[]{:S(2)}) %collective-permute-start) | collective-permute-done | bytes 1572896 | tf_op jit(solution)/shard_map/ppermute | solution.py:13
  145.2 6.0 %exponential_reduce_fusion.1 = (f32[16,384]{1,0:T(8,128)S(1)}, f32[16,384]{1,0:T(8,128)S(1)}, f32[16,384]{1,0:T(8,128)S(1)}) fusion(f32[16,384,384]{1,2,0:T(8,128)S(1)} %get-tuple-element.24, f32[16,384]{1,0:T(8,128)S(1)} %maximum_maximum_fusion, pred[]{:T(512)S(6)} %ge.26, f32[16,384,384]{1,2,0:T(8,128)S(1)} %get-tuple-element.20, pred[]{:T(512)S(6)} %ge.27, ...), kind=kLoop, calls=%fused_computation.8 | loop fusion | flops 28293120 | bytes 28557314 | tf_op jit(solution)/shard_map/reduce_sum | solution.py:73
  151.3 7.4 %fusion.10 = bf16[4,384,512]{2,1,0:T(8,128)(2,1)} fusion(bf16[4,384,2048]{2,1,0:T(8,128)(2,1)} %all-gather.2.cloned.1.call-done, bf16[512,2048]{1,0:T(8,128)(2,1)S(1)} %copy-done), kind=kOutput, calls=%fused_computation.35 | convolution fusion | flops 3222011904 | bytes 9961472 | tf_op jit(solution)/shard_map/btd,fd->btf/dot_general | solution.py:47
  163.7 8.1 %fusion.19 = f32[16,384,128]{1,2,0:T(8,128)} fusion(bf16[384,16,128]{0,2,1:T(8,128)(2,1)} %bitcast.128, f32[16,384,384]{1,2,0:T(8,128)} %copy-done.5, f32[16,384]{1,0:T(8,128)S(1)} %log_add_fusion, pred[]{:T(512)S(6)} %ge.26), kind=kOutput, calls=%fused_computation.42 | convolution fusion | flops 613416960 | bytes 14180353 | tf_op jit(solution)/shard_map/hts,shd->thd/dot_general | solution.py:82
  171.8 8.0 %fusion.22 = f32[16,384,128]{1,2,0:T(8,128)} fusion(bf16[384,16,128]{0,2,1:T(8,128)(2,1)S(1)} %bitcast.126, f32[16,384,384]{1,2,0:T(8,128)} %get-tuple-element.22, f32[16,384]{1,0:T(8,128)S(1)} %log_add_fusion, pred[384,384]{0,1:T(8,128)(4,1)S(1)} %iota_compare_fusion), kind=kOutput, calls=%fused_computation.43 | convolution fusion | flops 613416960 | bytes 14327808 | tf_op jit(solution)/shard_map/hts,shd->thd/dot_general | solution.py:82
  183.6 9.2 %multiply_reduce_fusion = (f32[384,16]{0,1:T(8,128)S(1)}, bf16[16,384,128]{1,2,0:T(8,128)(2,1)S(1)}) fusion(bf16[384,16,128]{0,2,1:T(8,128)(2,1)} %bitcast.110, bf16[384,16,128]{0,2,1:T(8,128)(2,1)} %bitcast.108, f32[16,384,384]{1,2,0:T(8,128)} %copy-done.2, f32[16,384]{1,0:T(8,128)S(1)} %log_add_fusion, pred[]{:T(512)S(6)} %ge.27, ...), kind=kOutput, calls=%fused_computation.23 | convolution fusion | flops 618915840 | bytes 20496384 | tf_op jit(solution)/shard_map/hts,shd->thd/dot_general | solution.py:82
  192.9 6.8 %convolution_convert_fusion = bf16[2048,2048]{0,1:T(8,128)(2,1)} fusion(bf16[384,2048]{0,1:T(8,128)(2,1)S(1)} %bitcast.123, bf16[1,384,2048]{2,1,0:T(8,128)(2,1)S(1)} %copy-done.10), kind=kOutput, calls=%fused_computation.16 | convolution fusion | flops 3225419776 | bytes 11534336 | tf_op jit(solution)/shard_map/dot_general | solution.py:118
  199.7 17.9 %all-to-all-start.1 = ((bf16[32,2048,64]{1,2,0:T(8,128)(2,1)}), bf16[32,2048,64]{1,2,0:T(8,128)(2,1)}, u32[]{:S(2)}, u32[]{:S(2)}) async-start(bf16[32,2048,64]{1,2,0:T(8,128)(2,1)} %bitcast.107), calls=%async_computation.1 | async-start | bytes 16777216 | tf_op jit(solution)/shard_map/all_to_all | solution.py:23
  217.6 7.0 %convolution_convert_fusion.2 = bf16[16,128,384]{2,1,0:T(8,128)(2,1)} fusion(bf16[384,16,128]{0,2,1:T(8,128)(2,1)S(1)} %bitcast.113, f32[16,384,384]{1,2,0:T(8,128)} %copy-done.5, f32[16,384]{1,0:T(8,128)S(1)} %log_add_fusion, pred[]{:T(512)S(6)} %ge.26), kind=kOutput, calls=%fused_computation.28 | convolution fusion | flops 614203392 | bytes 12607489 | tf_op jit(solution)/shard_map/hts,thd->shd/dot_general | solution.py:109
  227.3 7.1 %convolution_convert_fusion.1 = bf16[16,128,384]{2,1,0:T(8,128)(2,1)} fusion(bf16[384,16,128]{0,2,1:T(8,128)(2,1)S(1)} %bitcast.114, f32[16,384,384]{1,2,0:T(8,128)} %copy-done.2, f32[16,384]{1,0:T(8,128)S(1)} %log_add_fusion, pred[]{:T(512)S(6)} %ge.27), kind=kOutput, calls=%fused_computation.27 | convolution fusion | flops 614203392 | bytes 12607489 | tf_op jit(solution)/shard_map/hts,thd->shd/dot_general | solution.py:109
  244.6 7.8 %fusion.9 = f32[16,128,384]{2,1,0:T(8,128)} fusion(bf16[384,16,128]{0,2,1:T(8,128)(2,1)S(1)} %bitcast.115, f32[16,384,384]{1,2,0:T(8,128)} %get-tuple-element.22, f32[16,384]{1,0:T(8,128)S(1)} %log_add_fusion, pred[384,384]{0,1:T(8,128)(4,1)S(1)} %iota_compare_fusion), kind=kOutput, calls=%fused_computation.34 | convolution fusion | flops 614989824 | bytes 14327808 | tf_op jit(solution)/shard_map/hts,thd->shd/dot_general | solution.py:109
  256.3 7.8 %multiply_convert_fusion = bf16[16,384,384]{1,2,0:T(8,128)(2,1)S(1)} fusion(f32[16,384,384]{1,2,0:T(8,128)} %copy-done.2, f32[16,384]{1,0:T(8,128)S(1)} %bitcast.132, f32[16,384]{1,0:T(8,128)S(1)} %log_add_fusion, pred[]{:T(512)S(6)} %ge.27, bf16[384,16,128]{0,2,1:T(8,128)(2,1)} %bitcast.111, bf16[384,16,128]{0,2,1:T(8,128)(2,1)} %bitcast.109), kind=kOutput, calls=%fused_computation.1 | convolution fusion | flops 620494848 | bytes 17350656 | tf_op jit(solution)/shard_map/thd,shd->hts/dot_general | solution.py:96
  269.6 7.7 %multiply_convert_fusion.1 = bf16[16,384,384]{1,2,0:T(8,128)(2,1)S(1)} fusion(f32[16,384,384]{1,2,0:T(8,128)} %copy-done.5, f32[16,384]{1,0:T(8,128)S(1)} %bitcast.133, f32[16,384]{1,0:T(8,128)S(1)} %log_add_fusion, pred[]{:T(512)S(6)} %ge.26, bf16[384,16,128]{0,2,1:T(8,128)(2,1)} %bitcast.112, bf16[384,16,128]{0,2,1:T(8,128)(2,1)} %bitcast.129), kind=kOutput, calls=%fused_computation.2 | convolution fusion | flops 620494848 | bytes 17350656 | tf_op jit(solution)/shard_map/thd,shd->hts/dot_general | solution.py:96
  286.9 6.4 %multiply_convert_fusion.2 = bf16[16,384,384]{1,2,0:T(8,128)(2,1)S(1)} fusion(f32[16,384,384]{1,2,0:T(8,128)} %get-tuple-element.22, f32[16,384]{1,0:T(8,128)S(1)} %bitcast.134, f32[16,384]{1,0:T(8,128)S(1)} %log_add_fusion, pred[384,384]{0,1:T(8,128)(4,1)S(1)} %iota_compare_fusion, bf16[384,16,128]{0,2,1:T(8,128)(2,1)S(1)} %bitcast.127, ...), kind=kOutput, calls=%fused_computation.3 | convolution fusion | flops 620494848 | bytes 17498112 | tf_op jit(solution)/shard_map/thd,shd->hts/dot_general | solution.py:96
  306.9 5.6 %fusion.8 = f32[16,384,128]{1,2,0:T(8,128)} fusion(bf16[16,384,384]{1,2,0:T(8,128)(2,1)} %copy-done.7, bf16[384,16,128]{0,2,1:T(8,128)(2,1)S(1)} %bitcast.97), kind=kOutput, calls=%fused_computation.33 | convolution fusion | flops 605552640 | bytes 9437184 | tf_op jit(solution)/shard_map/hts,thd->shd/dot_general | solution.py:104
  316.1 51.4 %collective-permute-done.7 = bf16[384,2048]{1,0:T(8,128)(2,1)} collective-permute-done((bf16[384,2048]{1,0:T(8,128)(2,1)}, bf16[384,2048]{1,0:T(8,128)(2,1)}, u32[]{:S(2)}, u32[]{:S(2)}) %collective-permute-start.7) | collective-permute-done | bytes 1572896 | tf_op jit(solution)/shard_map/ppermute | solution.py:13
  367.5 14.0 %collective-permute-done.6 = bf16[384,2048]{1,0:T(8,128)(2,1)} collective-permute-done((bf16[384,2048]{1,0:T(8,128)(2,1)}, bf16[384,2048]{1,0:T(8,128)(2,1)}, u32[]{:S(2)}, u32[]{:S(2)}) %collective-permute-start.6) | collective-permute-done | bytes 1572896 | tf_op jit(solution)/shard_map/ppermute | solution.py:13
  386.3 5.6 %convert_reduce_fusion = f32[2048,64]{0,1:T(8,128)S(1)} fusion(bf16[32,2048,64]{1,2,0:T(8,128)(2,1)} %all-to-all-done.1), kind=kLoop, calls=%fused_computation | loop fusion | flops 8257536 | bytes 8912896 | tf_op jit(solution)/shard_map/reduce_sum | solution.py:24
  392.7 7.9 %all-to-all-start.2 = ((f32[4,512,64]{1,2,0:T(8,128)}), f32[4,512,64]{1,2,0:T(8,128)S(1)}, u32[]{:S(2)}, u32[]{:S(2)}) async-start(f32[4,512,64]{1,2,0:T(8,128)} %bitcast.90), calls=%async_computation.2 | async-start | bytes 1048576 | tf_op jit(solution)/shard_map/all_to_all | solution.py:29
  400.6 14.7 %collective-permute-done.4 = bf16[384,2048]{1,0:T(8,128)(2,1)} collective-permute-done((bf16[384,2048]{1,0:T(8,128)(2,1)}, bf16[384,2048]{1,0:T(8,128)(2,1)}, u32[]{:S(2)}, u32[]{:S(2)}) %collective-permute-start.4) | collective-permute-done | bytes 1572896 | tf_op jit(solution)/shard_map/ppermute | solution.py:13
  415.3 52.2 %collective-permute-done.5 = bf16[384,2048]{1,0:T(8,128)(2,1)} collective-permute-done((bf16[384,2048]{1,0:T(8,128)(2,1)}, bf16[384,2048]{1,0:T(8,128)(2,1)}, u32[]{:S(2)}, u32[]{:S(2)}) %collective-permute-start.5) | collective-permute-done | bytes 1572896 | tf_op jit(solution)/shard_map/ppermute | solution.py:13
  (87 shorter events, 107.9 us)
Async XLA Ops:
  7.2 144.1 %copy-start = (bf16[512,2048]{1,0:T(8,128)(2,1)S(1)}, bf16[512,2048]{1,0:T(8,128)(2,1)}, u32[]{:S(2)}) copy-start(bf16[512,2048]{1,0:T(8,128)(2,1)} %param.10) | copy-start | bytes 6291460
  7.2 144.1 %all-gather.2.cloned.1.call-start = ((), (), s32[]{:S(2)}) async-start(), calls=%async_computation.3 | async-start | bytes 7864320 | tf_op jit(solution)/shard_map/all_gather | solution.py:46
  10.8 39.5 %collective-permute-start.3 = (bf16[384,2048]{1,0:T(8,128)(2,1)}, bf16[384,2048]{1,0:T(8,128)(2,1)}, u32[]{:S(2)}, u32[]{:S(2)}) collective-permute-start(bf16[384,2048]{1,0:T(8,128)(2,1)} %bitcast.124), channel_id=1, source_target_pairs={{0,8},{4,12},{8,16},{12,20},{16,24},{20,28},{24,32},{28,36},{32,40... | collective-permute-start | bytes 4718600 | tf_op jit(solution)/shard_map/ppermute | solution.py:13
  13.6 72.9 %collective-permute-start.2 = (bf16[384,2048]{1,0:T(8,128)(2,1)}, bf16[384,2048]{1,0:T(8,128)(2,1)}, u32[]{:S(2)}, u32[]{:S(2)}) collective-permute-start(bf16[384,2048]{1,0:T(8,128)(2,1)} %bitcast.125), channel_id=1, source_target_pairs={{0,4},{4,8},{8,12},{12,16},{16,20},{20,24},{24,28},{28,32},{32,36}... | collective-permute-start | bytes 4718600 | tf_op jit(solution)/shard_map/ppermute | solution.py:13
  21.0 115.3 %collective-permute-start = (bf16[384,2048]{0,1:T(8,128)(2,1)}, bf16[384,2048]{0,1:T(8,128)(2,1)}, u32[]{:S(2)}, u32[]{:S(2)}) collective-permute-start(bf16[384,2048]{0,1:T(8,128)(2,1)} %bitcast.102), channel_id=1, source_target_pairs={{0,4},{4,8},{8,12},{12,16},{16,20},{20,24},{24,28},{28,32},{32,36}... | collective-permute-start | bytes 4718600 | tf_op jit(solution)/shard_map/ppermute | solution.py:13
  24.5 115.5 %collective-permute-start.1 = (bf16[384,2048]{0,1:T(8,128)(2,1)}, bf16[384,2048]{0,1:T(8,128)(2,1)}, u32[]{:S(2)}, u32[]{:S(2)}) collective-permute-start(bf16[384,2048]{0,1:T(8,128)(2,1)} %bitcast.103), channel_id=1, source_target_pairs={{0,8},{4,12},{8,16},{12,20},{16,24},{20,28},{24,32},{28,36},{32,40... | collective-permute-start | bytes 4718600 | tf_op jit(solution)/shard_map/ppermute | solution.py:13
  136.4 8.8 %slice-start = ((s8[9437184]{0:T(1024)(128)(4,1)}), s8[4194304]{0:T(1024)(128)(4,1)S(1)}, s32[]{:S(2)}) async-start(s8[9437184]{0:T(1024)(128)(4,1)} %bitcast.98), calls=%async_computation.4 | async-start | bytes 8388608
  136.4 8.8 %slice-start.1 = ((s8[9437184]{0:T(1024)(128)(4,1)}), s8[4194304]{0:T(1024)(128)(4,1)S(1)}, s32[]{:S(2)}) async-start(s8[9437184]{0:T(1024)(128)(4,1)} %bitcast.98), calls=%async_computation.5 | async-start | bytes 8388608
  145.1 6.0 %copy-start.2 = (f32[16,384,384]{1,2,0:T(8,128)}, f32[16,384,384]{1,2,0:T(8,128)S(1)}, u32[]{:S(2)}) copy-start(f32[16,384,384]{1,2,0:T(8,128)S(1)} %get-tuple-element.20) | copy-start | bytes 28311556
  158.7 23.4 %all-to-all-start = ((bf16[4,384,512]{2,1,0:T(8,128)(2,1)}), bf16[4,384,512]{2,1,0:T(8,128)(2,1)S(1)}, u32[]{:S(2)}, u32[]{:S(2)}) async-start(bf16[4,384,512]{2,1,0:T(8,128)(2,1)} %fusion.10), calls=%async_computation | async-start | bytes 3145728 | tf_op jit(solution)/shard_map/all_to_all | solution.py:50
  163.7 8.1 %copy-start.13 = (bf16[1,384,2048]{1,2,0:T(8,128)(2,1)S(1)}, bf16[1,384,2048]{1,2,0:T(8,128)(2,1)}, u32[]{:S(2)}) copy-start(bf16[1,384,2048]{1,2,0:T(8,128)(2,1)} %copy.165) | copy-start | bytes 4718596
  183.6 9.3 %copy-start.10 = (bf16[1,384,2048]{2,1,0:T(8,128)(2,1)S(1)}, bf16[1,384,2048]{2,1,0:T(8,128)(2,1)}, u32[]{:S(2)}) copy-start(bf16[1,384,2048]{2,1,0:T(8,128)(2,1)} %broadcast_multiply_fusion) | copy-start | bytes 4718596
  199.7 17.9 %copy-start.11 = (bf16[1,384,4,512]{1,3,2,0:T(8,128)(2,1)S(1)}, bf16[1,384,4,512]{1,3,2,0:T(8,128)(2,1)}, u32[]{:S(2)}) copy-start(bf16[1,384,4,512]{1,3,2,0:T(8,128)(2,1)} %copy.104) | copy-start | bytes 4718596
  199.7 186.5 %all-to-all-start.1 = ((bf16[32,2048,64]{1,2,0:T(8,128)(2,1)}), bf16[32,2048,64]{1,2,0:T(8,128)(2,1)}, u32[]{:S(2)}, u32[]{:S(2)}) async-start(bf16[32,2048,64]{1,2,0:T(8,128)(2,1)} %bitcast.107), calls=%async_computation.1 | async-start | bytes 16777216 | tf_op jit(solution)/shard_map/all_to_all | solution.py:23
  237.0 130.5 %collective-permute-start.7 = (bf16[384,2048]{1,0:T(8,128)(2,1)}, bf16[384,2048]{1,0:T(8,128)(2,1)}, u32[]{:S(2)}, u32[]{:S(2)}) collective-permute-start(bf16[384,2048]{1,0:T(8,128)(2,1)} %copy.138), channel_id=1, source_target_pairs={{8,0},{12,4},{16,8},{20,12},{24,16},{28,20},{32,24},{36,28},{40,32... | collective-permute-start | bytes 4718600 | tf_op jit(solution)/shard_map/ppermute | solution.py:13
  239.8 141.8 %collective-permute-start.6 = (bf16[384,2048]{1,0:T(8,128)(2,1)}, bf16[384,2048]{1,0:T(8,128)(2,1)}, u32[]{:S(2)}, u32[]{:S(2)}) collective-permute-start(bf16[384,2048]{1,0:T(8,128)(2,1)} %copy.135), channel_id=1, source_target_pairs={{4,0},{8,4},{12,8},{16,12},{20,16},{24,20},{28,24},{32,28},{36,32}... | collective-permute-start | bytes 4718600 | tf_op jit(solution)/shard_map/ppermute | solution.py:13
  256.3 7.8 %copy-start.4 = (bf16[1,384,2048]{1,2,0:T(8,128)(2,1)S(1)}, bf16[1,384,2048]{1,2,0:T(8,128)(2,1)}, u32[]{:S(2)}) copy-start(bf16[1,384,2048]{1,2,0:T(8,128)(2,1)} %copy.164) | copy-start | bytes 4718596
  282.7 12.8 %slice-start.3 = ((s8[4718592]{0:T(1024)(128)(4,1)}), s8[4194304]{0:T(1024)(128)(4,1)S(1)}, s32[]{:S(2)}) async-start(s8[4718592]{0:T(1024)(128)(4,1)} %bitcast.100), calls=%async_computation.7 | async-start | bytes 8388608
  286.9 6.4 %copy-start.9 = (bf16[1,384,2048]{1,2,0:T(8,128)(2,1)S(1)}, bf16[1,384,2048]{1,2,0:T(8,128)(2,1)}, u32[]{:S(2)}) copy-start(bf16[1,384,2048]{1,2,0:T(8,128)(2,1)} %copy.163) | copy-start | bytes 4718596
  286.9 8.6 %slice-start.4 = ((s8[4718592]{0:T(1024)(128)(4,1)}), s8[524288]{0:T(1024)(128)(4,1)S(1)}, s32[]{:S(2)}) async-start(s8[4718592]{0:T(1024)(128)(4,1)} %bitcast.100), calls=%async_computation.8 | async-start | bytes 1048576
  302.0 113.3 %collective-permute-start.4 = (bf16[384,2048]{1,0:T(8,128)(2,1)}, bf16[384,2048]{1,0:T(8,128)(2,1)}, u32[]{:S(2)}, u32[]{:S(2)}) collective-permute-start(bf16[384,2048]{1,0:T(8,128)(2,1)} %copy.128), channel_id=1, source_target_pairs={{4,0},{8,4},{12,8},{16,12},{20,16},{24,20},{28,24},{32,28},{36,32}... | collective-permute-start | bytes 4718600 | tf_op jit(solution)/shard_map/ppermute | solution.py:13
  304.5 163.1 %collective-permute-start.5 = (bf16[384,2048]{1,0:T(8,128)(2,1)}, bf16[384,2048]{1,0:T(8,128)(2,1)}, u32[]{:S(2)}, u32[]{:S(2)}) collective-permute-start(bf16[384,2048]{1,0:T(8,128)(2,1)} %copy.132), channel_id=1, source_target_pairs={{8,0},{12,4},{16,8},{20,12},{24,16},{28,20},{32,24},{36,28},{40,32... | collective-permute-start | bytes 4718600 | tf_op jit(solution)/shard_map/ppermute | solution.py:13
  392.7 79.6 %all-to-all-start.2 = ((f32[4,512,64]{1,2,0:T(8,128)}), f32[4,512,64]{1,2,0:T(8,128)S(1)}, u32[]{:S(2)}, u32[]{:S(2)}) async-start(f32[4,512,64]{1,2,0:T(8,128)} %bitcast.90), calls=%async_computation.2 | async-start | bytes 1048576 | tf_op jit(solution)/shard_map/all_to_all | solution.py:29
  400.6 72.4 %copy-start.1 = (bf16[512,2048]{1,0:T(8,128)(2,1)S(1)}, bf16[512,2048]{1,0:T(8,128)(2,1)}, u32[]{:S(2)}) copy-start(bf16[512,2048]{1,0:T(8,128)(2,1)} %param.10) | copy-start | bytes 6291460
  (8 other events, 30.2 us)
Sparse Core Ops, SparseCore 0:
  10.9 115.3 all-gather.1
where the time goes:
time: 489 us; the launch traced here: 480 us
  waiting for transfers between devices  225 us (46%)
  matrix products  120 us (25%)
  starting transfers between devices  57.9 us (12%)
  local copies, waits for them, and re-layouts  36.9 us (8%)
  other arithmetic  24.5 us (5%)
  between operations  15.7 us (3%)
    ppermute x8, waiting for transfers between devices, from_behind(): return lax.ppermute(block, axis, route)  223 us
    ppermute x8, starting transfers between devices, from_behind(): return lax.ppermute(block, axis, route)  27.2 us
    dot_general x3, matrix products, per_device(): jnp.einsum('hts,shd->thd', probs_b, value_heads, preferred_element_type=j...  25.3 us
    dot_general x3, matrix products, per_device(): jnp.einsum('thd,shd->hts', out_heads, value_heads, preferred_element_type...  22 us
    dot_general x3, matrix products, per_device(): jnp.einsum('hts,thd->shd', probs_b, out_heads, preferred_element_type=jnp...  22 us
    all_to_all x1, starting transfers between devices, sum_at_owner(): lax.all_to_all(pieces, axis, split_axis=0, concat_axis=0, tiled=True)  17.9 us
    dot_general x3, matrix products, per_device(): jnp.einsum('thd,shd->hts', query_heads, key_heads, preferred_element_type...  16.1 us
    dot_general x3, matrix products, per_device(): jnp.einsum('hts,thd->shd', score_grad, query_heads, preferred_element_typ...  11.1 us
  transfers between devices with their start and end apart: 12, of which 8 were waited for; matrix products, arithmetic and copies ran while one was open for 32% of the time, Pallas kernels for 0%

commit v1 on v0

v1 whole, which is shorter than its diff:
```python
import functools

import jax
import jax.numpy as jnp
from jax import lax
from jax.experimental import pallas as pl
from jax.experimental.pallas import tpu as pltpu
from jax.sharding import PartitionSpec as P

HEAD_DIM = 128
LOG2E = 1.4426950408889634
MESH = pl.DeviceIdType.MESH

AB = (((1,), (0,)), ((), ()))
ABT = (((1,), (1,)), ((), ()))


def mm(left, right, dims):
    return lax.dot_general(left, right, dims, preferred_element_type=jnp.float32)


def attention_kernel(
    q_ref,
    k_ref,
    v_ref,
    g_ref,
    w_ref,
    dq_ref,
    dk_ref,
    dv_ref,
    wg_ref,
    q_buf,
    k_buf,
    v_buf,
    g_buf,
    w_buf,
    do_buf,
    at_buf,
    dq_buf,
    kh_buf,
    vh_buf,
    kr_buf,
    vr_buf,
    ko_buf,
    vo_buf,
    kf_buf,
    vf_buf,
    zs_sem,
    kz_sem,
    vz_sem,
    qz_sem,
    g_sem,
    gx_sem,
    w_sem,
    wl_sem,
    ys_sem,
    ky_sem,
    vy_sem,
    rs_sem,
    kr_sem,
    vr_sem,
    os_sem,
    o_sem,
):
    seq = lax.axis_index("seq")
    dp = lax.axis_index("dp")
    columns = lax.axis_size("seq") // 2
    zh = lax.rem(seq, 2)
    col = lax.div(seq, 2)
    zl = lax.div(dp, 2)
    core = lax.rem(dp, 2)
    tokens = q_ref.shape[1]
    half = q_ref.shape[2] // 2
    heads = half // HEAD_DIM
    quarter = w_ref.shape[0]
    scale = HEAD_DIM ** (-0.5)

    def device(col_, zh_, zl_, core_):
        return (2 * col_ + zh_, 2 * zl_ + core_)

    targets = [device(col, core, 1 - zl, t) for t in range(2)]
    homes = [device(col, b, 1 - zl, zh) for b in range(2)]
    following = device(lax.rem(col + 1, columns), zh, zl, core)
    previous = device(lax.rem(col + columns - 1, columns), zh, zl, core)
    partner = device(col, zh, zl, 1 - core)

    barrier = pltpu.get_barrier_semaphore()
    greeted = [following, previous]
    for i in range(1, 8):
        greeted.append(
            device(
                col,
                1 - zh if i & 4 else zh,
                1 - zl if i & 2 else zl,
                1 - core if i & 1 else core,
            )
        )
    for other in greeted:
        pl.semaphore_signal(barrier, inc=1, device_id=other, device_id_type=MESH)
    pl.semaphore_wait(barrier, len(greeted))

    def remote(src, dst, send_sem, recv_sem, to):
        return pltpu.make_async_remote_copy(
            src_ref=src,
            dst_ref=dst,
            send_sem=send_sem,
            recv_sem=recv_sem,
            device_id=to,
            device_id_type=MESH,
        )

    def lanes(h):
        return pl.ds(pl.multiple_of(h * HEAD_DIM, HEAD_DIM), HEAD_DIM)

    my_rows = pl.ds(pl.multiple_of(zh * tokens, tokens), tokens)
    own_rows = pl.ds(2 * tokens, 2 * tokens)
    halo_rows = pl.ds(0, 2 * tokens)
    my_half = pl.ds(pl.multiple_of(core * half, half), half)

    def send_home(ref, buf, base, h, recv_sem, slot):
        rows = pl.ds(pl.multiple_of(base + zh * tokens, tokens), tokens)
        for t in range(2):
            src = pl.ds(pl.multiple_of(t * half + h * HEAD_DIM, HEAD_DIM), HEAD_DIM)
            remote(
                ref.at[0, :, src],
                buf.at[rows, lanes(h)],
                zs_sem.at[slot],
                recv_sem.at[h],
                targets[t],
            ).start()

    send_home(k_ref, k_buf, 2 * tokens, 0, kz_sem, 0)
    send_home(v_ref, v_buf, 2 * tokens, 0, vz_sem, 1)
    for t in range(2):
        cols = pl.ds(t * half, half)
        remote(
            g_ref.at[:, cols],
            g_buf.at[my_rows, cols],
            zs_sem.at[3],
            g_sem,
            targets[t],
        ).start()
    w_rows = pl.ds(pl.multiple_of(core * quarter, quarter), quarter)
    w_local = pltpu.make_async_copy(w_ref, w_buf.at[w_rows], wl_sem)

    def w_send(to):
        return remote(w_ref, w_buf.at[w_rows], zs_sem.at[4], w_sem, to)

    w_far = [device(col, b, 1 - zl, zl) for b in range(2)]

    @pl.when(core == zl)
    def _():
        w_local.start()

    @pl.when(core != zl)
    def _():
        w_send(partner).start()

    @pl.when(zh == core)
    def _():
        for to in w_far:
            w_send(to).start()

    send_home(q_ref, q_buf, 0, 0, qz_sem, 2)

    @pl.loop(1, heads)
    def _(h):
        send_home(k_ref, k_buf, 2 * tokens, h, kz_sem, 0)
        send_home(v_ref, v_buf, 2 * tokens, h, vz_sem, 1)
        send_home(q_ref, q_buf, 0, h, qz_sem, 2)

    def forward(h):
        for buf, got, sem, slot in (
            (k_buf, kz_sem, ky_sem, 0),
            (v_buf, vz_sem, vy_sem, 1),
        ):
            own = buf.at[own_rows, lanes(h)]
            remote(own, own, zs_sem.at[0], got.at[h], partner).wait_recv()
            remote(own, buf.at[halo_rows, lanes(h)], ys_sem.at[slot], sem.at[h], following).start()

    forward(0)

    g_half = g_buf.at[:, my_half]
    remote(g_half, g_half, zs_sem.at[3], g_sem, partner).wait_recv()
    g_swap = remote(g_half, g_half, zs_sem.at[5], gx_sem, partner)
    g_swap.start()

    @pl.when(core == zl)
    def _():
        w_local.wait()
        w_send(partner).wait_recv()

    @pl.when(core != zl)
    def _():
        remote(w_buf, w_buf, zs_sem.at[4], w_sem, partner).wait_recv()

    g_swap.wait_recv()

    @pl.loop(0, 2 * tokens // 256)
    def _(n):
        rows = pl.ds(pl.multiple_of(n * 256, 256), 256)
        do_buf[:, rows] = mm(w_buf[...], g_buf[rows, :], ABT).astype(jnp.bfloat16)

    first = jnp.where(col == 0, -1e30, 0.0).astype(jnp.float32)
    key_pos = lax.broadcasted_iota(jnp.int32, (tokens, tokens), 0)
    query_pos = lax.broadcasted_iota(jnp.int32, (tokens, tokens), 1)

    def head(h):
        at = lanes(h)
        feats = pl.ds(pl.multiple_of(h * HEAD_DIM, HEAD_DIM), HEAD_DIM)
        value_t = v_buf[:, at].T
        key_t = k_buf[:, at].T
        dk = [None] * 4
        dv = [None] * 4

        def add(total, block, term):
            total[block] = term if total[block] is None else total[block] + term

        for b in range(2):
            rows = slice(b * tokens, (b + 1) * tokens)
            q = q_buf[rows, at]
            do = do_buf[feats, rows]
            blocks = [b, b + 1, b + 2]
            tile = [slice(n * tokens, (n + 1) * tokens) for n in blocks]
            scores = []
            for j in range(3):
                s = mm(k_buf[tile[j], at], q, ABT)
                if blocks[j] < 2:
                    s = s + first
                if j == 2:
                    s = jnp.where(key_pos <= query_pos, s, -1e30)
                scores.append(s)
            top = scores[0].max(axis=0, keepdims=True)
            for s in scores[1:]:
                top = jnp.maximum(top, s.max(axis=0, keepdims=True))
            probs = [jnp.exp2((s - top) * (scale * LOG2E)) for s in scores]
            total = probs[0].sum(axis=0, keepdims=True)
            for p in probs[1:]:
                total = total + p.sum(axis=0, keepdims=True)
            inverse = 1.0 / total
            probs = [p * inverse for p in probs]
            attn = None
            for j in range(3):
                probs_b = probs[j].astype(jnp.bfloat16)
                term = mm(value_t[:, tile[j]], probs_b, AB)
                attn = term if attn is None else attn + term
                add(dv, blocks[j], mm(probs_b, do, ABT))
            attn = attn.astype(jnp.bfloat16)
            at_buf[feats, rows] = attn
            delta = jnp.sum(
                do.astype(jnp.float32) * attn.astype(jnp.float32), axis=0, keepdims=True
            )
            dq = None
            for j in range(3):
                grad = mm(v_buf[tile[j], at], do, AB)
                sg = (probs[j] * (grad - delta)).astype(jnp.bfloat16)
                term = mm(key_t[:, tile[j]], sg, AB)
                dq = term if dq is None else dq + term
                add(dk, blocks[j], mm(sg, q, AB))
            dq_buf[rows, at] = (dq * scale).T.astype(jnp.bfloat16)
        for n in range(2):
            rows = slice(n * tokens, (n + 1) * tokens)
            kh_buf[rows, at] = (dk[n] * scale).astype(jnp.bfloat16)
            vh_buf[rows, at] = dv[n].astype(jnp.bfloat16)
            ko_buf[rows, at] = dk[n + 2] * scale
            vo_buf[rows, at] = dv[n + 2]

    def send_out(buf, out, slot, h):
        cols = pl.ds(pl.multiple_of(core * half + h * HEAD_DIM, HEAD_DIM), HEAD_DIM)
        for b in range(2):
            remote(
                buf.at[pl.ds(b * tokens, tokens), lanes(h)],
                out.at[0, :, cols],
                os_sem.at[slot],
                o_sem.at[slot],
                homes[b],
            ).start()

    def finish(h):
        at = lanes(h)
        for got, own, done, out, sem, slot in (
            (kr_buf, ko_buf, kf_buf, dk_ref, kr_sem, 1),
            (vr_buf, vo_buf, vf_buf, dv_ref, vr_sem, 2),
        ):
            piece = got.at[:, at]
            remote(piece, piece, rs_sem.at[0], sem.at[h], partner).wait_recv()
            done[:, at] = (own[:, at] + got[:, at].astype(jnp.float32)).astype(jnp.bfloat16)
            send_out(done, out, slot, h)

    @pl.loop(0, heads)
    def _(h):
        @pl.when(h + 1 < heads)
        def _():
            forward(h + 1)

        at = lanes(h)
        piece = q_buf.at[:, at]
        remote(piece, piece, zs_sem.at[2], qz_sem.at[h], partner).wait_recv()
        for buf, sem in ((k_buf, ky_sem), (v_buf, vy_sem)):
            piece = buf.at[halo_rows, at]
            remote(piece, piece, ys_sem.at[0], sem.at[h], partner).wait_recv()
        head(h)
        for src, dst, sem, slot in ((kh_buf, kr_buf, kr_sem, 0), (vh_buf, vr_buf, vr_sem, 1)):
            remote(
                src.at[:, at], dst.at[:, at], rs_sem.at[slot], sem.at[h], previous
            ).start()
        send_out(dq_buf, dq_ref, 0, h)

        @pl.when(h >= 2)
        def _():
            finish(h - 2)

    @pl.loop(0, wg_ref.shape[1] // 256)
    def _(n):
        cols = pl.ds(pl.multiple_of(n * 256, 256), 256)
        wg_ref[:, cols] = mm(at_buf[...], g_buf[:, cols], AB).astype(jnp.bfloat16)

    finish(heads - 2)
    finish(heads - 1)

    for ref, slot in ((k_ref, 0), (v_ref, 1), (q_ref, 2)):
        remote(ref, ref, zs_sem.at[slot], o_sem.at[0], partner).wait_send()
    remote(g_ref, g_ref, zs_sem.at[3], o_sem.at[0], partner).wait_send()

    @pl.when(core != zl)
    def _():
        w_send(partner).wait_send()

    @pl.when(zh == core)
    def _():
        for to in w_far:
            w_send(to).wait_send()

    g_swap.wait_send()
    for buf, slot in ((kr_buf, 0), (vr_buf, 1)):
        remote(buf, buf, ys_sem.at[slot], o_sem.at[0], partner).wait_send()
        remote(buf, buf, rs_sem.at[slot], o_sem.at[0], partner).wait_send()
    for buf, out, slot in ((dq_buf, dq_ref, 0), (kf_buf, dk_ref, 1), (vf_buf, dv_ref, 2)):
        remote(buf, buf, os_sem.at[slot], o_sem.at[0], partner).wait_send()
        remote(out, out, os_sem.at[slot], o_sem.at[slot], partner).wait_recv()


def attention(queries, keys, values, grad_masked, proj_weight):
    tokens, width = queries.shape[1:]
    half = width // 2
    heads = half // HEAD_DIM
    grad_width = grad_masked.shape[1]
    any_space = pl.BlockSpec(memory_space=pl.ANY)
    dma = pltpu.SemaphoreType.DMA
    bf16 = jnp.bfloat16

    def vmem(rows, cols, dtype=bf16):
        return pltpu.VMEM((rows, cols), dtype)

    pair = vmem(2 * tokens, half)
    outs = jax.ShapeDtypeStruct(queries.shape, bf16)
    return pl.pallas_call(
        attention_kernel,
        out_shape=(outs, outs, outs, jax.ShapeDtypeStruct((half, grad_width), bf16)),
        in_specs=[any_space] * 5,
        out_specs=(any_space, any_space, any_space, pl.BlockSpec(memory_space=pltpu.VMEM)),
        scratch_shapes=[
            pair,
            vmem(4 * tokens, half),
            vmem(4 * tokens, half),
            vmem(2 * tokens, grad_width),
            vmem(half, grad_width),
            vmem(half, 2 * tokens),
            vmem(half, 2 * tokens),
            pair,
            pair,
            pair,
            pair,
            pair,
            vmem(2 * tokens, half, jnp.float32),
            vmem(2 * tokens, half, jnp.float32),
            pair,
            pair,
            dma((6,)),
            dma((heads,)),
            dma((heads,)),
            dma((heads,)),
            dma,
            dma,
            dma,
            dma,
            dma((2,)),
            dma((heads,)),
            dma((heads,)),
            dma((2,)),
            dma((heads,)),
            dma((heads,)),
            dma((3,)),
            dma((3,)),
        ],
        compiler_params=pltpu.CompilerParams(
            collective_id=0, has_side_effects=True, vmem_limit_bytes=66_000_000
        ),
        name="attention",
    )(queries, keys, values, grad_masked, proj_weight)


def reduce_weight(partial):
    blocks = lax.axis_size("seq")
    half, width = partial.shape
    pieces = jnp.moveaxis(partial.reshape(half, blocks, width // blocks), 1, 0)
    arrived = lax.all_to_all(pieces, "seq", split_axis=0, concat_axis=0, tiled=True)
    summed = arrived.astype(jnp.float32).sum(axis=0)
    core = lax.rem(lax.axis_index("dp"), 2)
    rows = summed.reshape(2, half // 2, width // blocks)
    none = jnp.zeros_like(rows)
    padded = jnp.concatenate(
        [jnp.where(core == 0, rows, none), jnp.where(core == 1, rows, none)], axis=0
    )
    parts = lax.all_to_all(padded, "dp", split_axis=0, concat_axis=0, tiled=True)
    return parts.sum(axis=0)


def per_device(queries, keys, values, out_grad, proj_weight, lengths):
    tokens = queries.shape[1]
    position = lax.axis_index("seq")
    query_pos = position * tokens + jnp.arange(tokens, dtype=jnp.int32)
    live = (query_pos < lengths[0]).astype(jnp.bfloat16)
    grad_masked = out_grad[0] * live[:, None]
    dq, dk, dv, partial = attention(queries, keys, values, grad_masked, proj_weight)
    return dq, dk, dv, reduce_weight(partial)


def solution(mesh):
    placed = (
        P("dp", "seq", None),
        P("dp", "seq", None),
        P("dp", "seq", None),
        P("dp", "seq", None),
        P("dp", None),
        P("dp"),
    )
    return jax.shard_map(
        per_device,
        mesh=mesh,
        in_specs=placed,
        out_specs=(
            P("dp", "seq", None),
            P("dp", "seq", None),
            P("dp", "seq", None),
            P("dp", "seq"),
        ),
        check_vma=False,
    )
```

time: 489 us -> 253 us (0.52)
  the two profiles are of different devices: /device:TPU:60 before, /device:TPU:1 now
where the time goes in v1:
time: 253 us
  Pallas kernels  154 us (61%)
  waiting for transfers between devices  69.1 us (27%)
  local copies, waits for them, and re-layouts  11.6 us (5%)
  starting transfers between devices  9.33 us (4%)
  other arithmetic  7.44 us (3%)
    pallas_call x1, Pallas kernels, attention(): pl.pallas_call(attention_kernel, out_shape=(outs, outs, outs, jax.ShapeDt...  154 us
    all_to_all x1, waiting for transfers between devices, reduce_weight(): lax.all_to_all(pieces, 'seq', split_axis=0, concat_axis=0, tiled=True)  61.2 us
    all_to_all x1, waiting for transfers between devices, reduce_weight(): lax.all_to_all(padded, 'dp', split_axis=0, concat_axis=0, tiled=True)  7.85 us
    pallas_call x1, local copies, waits for them, and re-layouts, attention(): pl.pallas_call(attention_kernel, out_shape=(outs, outs, outs, jax.ShapeDt...  6.44 us
    unnamed x9, local copies, waits for them, and re-layouts  5.1 us
  transfers between devices with their start and end apart: 2, of which 2 were waited for; matrix products, arithmetic and copies ran while one was open for 0% of the time, Pallas kernels for 0%

profile of v1, /device:TPU:1, one launch (start us, length us, event | category | flops | bytes accessed | tf_op | source)
XLA Modules:
  0.0 252.6 jit_solution(976286066484140701)
XLA Ops:
  1.3 2.7 %bitcast_multiply_fusion.g_ref = bf16[384,2048]{1,0:T(8,128)(2,1)} fusion(bf16[1,384,2048]{2,1,0:T(8,128)(2,1)} %param.9, bf16[384]{0:T(512)(128)(2,1)S(1)} %fusion), kind=kLoop, calls=%fused_computation.1 | loop fusion | flops 786432 | bytes 3146496 | tf_op jit(solution)/shard_map/mul | solution.py:424
  4.0 153.9 %attention.1 = (bf16[1,384,2048]{2,1,0:T(8,128)(2,1)}, bf16[1,384,2048]{2,1,0:T(8,128)(2,1)}, bf16[1,384,2048]{2,1,0:T(8,128)(2,1)}, bf16[1024,2048]{1,0:T(8,128)(2,1)}) custom-call(bf16[1,384,2048]{2,1,0:T(8,128)(2,1)} %q_ref.1, bf16[1,384,2048]{2,1,0:T(8,128)(2,1)} %k_ref.1, bf16[1,384,2048]{2,1,0:T(8,128)(2,1)} %v_ref.1, ...), custom_call_target="tpu_custom_call" | custom-call | tf_op jit(solution)/shard_map/attention/pallas_call | solution.py:357
  157.9 6.4 %copy.11 = bf16[1024,2048]{0,1:T(8,128)(2,1)} copy(bf16[1024,2048]{1,0:T(8,128)(2,1)} %get-tuple-element.11) | data formatting | bytes 8388608 | tf_op jit(solution)/shard_map/attention/pallas_call | solution.py:357
  164.3 4.9 %all-to-all-start = ((bf16[32,1024,64]{1,2,0:T(8,128)(2,1)}), bf16[32,1024,64]{1,2,0:T(8,128)(2,1)}, u32[]{:S(2)}, u32[]{:S(2)}) async-start(bf16[32,1024,64]{1,2,0:T(8,128)(2,1)} %bitcast.13), calls=%async_computation | async-start | bytes 8388608 | tf_op jit(solution)/shard_map/all_to_all | solution.py:407
  169.2 61.2 %all-to-all-done = bf16[32,1024,64]{1,2,0:T(8,128)(2,1)} async-done(((bf16[32,1024,64]{1,2,0:T(8,128)(2,1)}), bf16[32,1024,64]{1,2,0:T(8,128)(2,1)}, u32[]{:S(2)}, u32[]{:S(2)}) %all-to-all-start) | async-done | bytes 4194336 | tf_op jit(solution)/shard_map/all_to_all | solution.py:407
  230.4 3.1 %convert_reduce_fusion = f32[1024,64]{0,1:T(8,128)S(1)} fusion(bf16[32,1024,64]{1,2,0:T(8,128)(2,1)} %all-to-all-done), kind=kLoop, calls=%fused_computation | loop fusion | flops 4128768 | bytes 4456448 | tf_op jit(solution)/shard_map/reduce_sum | solution.py:408
  233.7 0.0 copy-start.2
  233.7 0.8 pad_maximum_fusion
  234.5 4.5 %all-to-all-start.1 = ((f32[4,512,64]{1,2,0:T(8,128)}), f32[4,512,64]{1,2,0:T(8,128)S(1)}, u32[]{:S(2)}, u32[]{:S(2)}) async-start(f32[4,512,64]{1,2,0:T(8,128)} %pad_maximum_fusion), calls=%async_computation.1 | async-start | bytes 1048576 | tf_op jit(solution)/shard_map/all_to_all | solution.py:415
  239.0 7.8 %all-to-all-done.1 = f32[4,512,64]{1,2,0:T(8,128)S(1)} async-done(((f32[4,512,64]{1,2,0:T(8,128)}), f32[4,512,64]{1,2,0:T(8,128)S(1)}, u32[]{:S(2)}, u32[]{:S(2)}) %all-to-all-start.1) | async-done | bytes 524320 | tf_op jit(solution)/shard_map/all_to_all | solution.py:415
  246.8 0.7 reduce_sum.19
  247.5 0.0 copy-done.2
  247.5 0.0 copy-start.1
  247.5 1.1 copy.22
  248.7 0.8 copy-done.1
  249.5 0.0 copy-start
  249.5 1.1 copy.23
  250.7 0.8 copy-done
  251.5 1.1 copy.24
  (3 shorter events, 0.1 us)
Async XLA Ops:
  164.3 66.1 %all-to-all-start = ((bf16[32,1024,64]{1,2,0:T(8,128)(2,1)}), bf16[32,1024,64]{1,2,0:T(8,128)(2,1)}, u32[]{:S(2)}, u32[]{:S(2)}) async-start(bf16[32,1024,64]{1,2,0:T(8,128)(2,1)} %bitcast.13), calls=%async_computation | async-start | bytes 8388608 | tf_op jit(solution)/shard_map/all_to_all | solution.py:407
  233.7 13.9 %copy-start.2 = (bf16[1,384,2048]{2,1,0:T(8,128)(2,1)S(1)}, bf16[1,384,2048]{2,1,0:T(8,128)(2,1)}, u32[]{:S(2)}) copy-start(bf16[1,384,2048]{2,1,0:T(8,128)(2,1)} %get-tuple-element.20) | copy-start | bytes 4718596
  234.5 12.3 %all-to-all-start.1 = ((f32[4,512,64]{1,2,0:T(8,128)}), f32[4,512,64]{1,2,0:T(8,128)S(1)}, u32[]{:S(2)}, u32[]{:S(2)}) async-start(f32[4,512,64]{1,2,0:T(8,128)} %pad_maximum_fusion), calls=%async_computation.1 | async-start | bytes 1048576 | tf_op jit(solution)/shard_map/all_to_all | solution.py:415
  247.5 2.0 copy-start.1
  249.5 2.0 copy-start

commit v2 on v1

--- a/solution.py
+++ b/solution.py
@@ -1,5 +1,3 @@
-import functools
-
 import jax
 import jax.numpy as jnp
 from jax import lax
@@ -25,6 +23,7 @@
     v_ref,
     g_ref,
     w_ref,
+    len_ref,
     dq_ref,
     dk_ref,
     dv_ref,
@@ -45,6 +44,20 @@
     vo_buf,
     kf_buf,
     vf_buf,
+    gm_buf,
+    p_buf,
+    x1_buf,
+    x2_buf,
+    y1_buf,
+    y2_buf,
+    zr_buf,
+    gl_sem,
+    px_sem,
+    x1_sem,
+    x2_sem,
+    y1_sem,
+    y2_sem,
+    zr_sem,
     zs_sem,
     kz_sem,
     vz_sem,
@@ -84,8 +97,26 @@
     previous = device(lax.rem(col + columns - 1, columns), zh, zl, core)
     partner = device(col, zh, zl, 1 - core)
 
+    g_local = pltpu.make_async_copy(g_ref.at[0], gm_buf, gl_sem)
+    g_local.start()
+
+    x_at = lax.div(col, 4)
+    y_at = lax.rem(col, 4)
+
+    def pair_of(at, step):
+        near = at + 1 - 2 * lax.rem(at, 2)
+        turned = lax.rem(core + step, 2)
+        return jnp.where(turned == 0, near, 3 - at)
+
+    x_pair = [pair_of(x_at, step) for step in range(2)]
+    y_pair = [pair_of(y_at, step) for step in range(2)]
+    x_far = lax.rem(x_at + 2, 4)
+    y_far = lax.rem(y_at + 2, 4)
+    x_dev = [device(4 * n + y_at, zh, zl, core) for n in x_pair]
+    y_dev = [device(4 * x_at + n, zh, zl, core) for n in y_pair]
+
     barrier = pltpu.get_barrier_semaphore()
-    greeted = [following, previous]
+    greeted = [following, previous, *x_dev, *y_dev]
     for i in range(1, 8):
         greeted.append(
             device(
@@ -131,10 +162,14 @@
 
     send_home(k_ref, k_buf, 2 * tokens, 0, kz_sem, 0)
     send_home(v_ref, v_buf, 2 * tokens, 0, vz_sem, 1)
+    g_local.wait()
+    limit = len_ref[0] - seq * tokens
+    live = lax.broadcasted_iota(jnp.int32, gm_buf.shape, 0) < limit
+    gm_buf[...] = jnp.where(live, gm_buf[...], jnp.zeros_like(gm_buf))
     for t in range(2):
         cols = pl.ds(t * half, half)
         remote(
-            g_ref.at[:, cols],
+            gm_buf.at[:, cols],
             g_buf.at[my_rows, cols],
             zs_sem.at[3],
             g_sem,
@@ -287,6 +322,120 @@
             done[:, at] = (own[:, at] + got[:, at].astype(jnp.float32)).astype(jnp.bfloat16)
             send_out(done, out, slot, h)
 
+    group = 2 * HEAD_DIM
+    groups = half // group
+    part = wg_ref.shape[1] * 8
+
+    def group_rows(n):
+        return pl.ds(pl.multiple_of(n * group, group), group)
+
+    def columns_of(n, size):
+        return pl.ds(pl.multiple_of(n * size, size), size)
+
+    def f32(value):
+        return value.astype(jnp.float32)
+
+    def product(n):
+        rows = group_rows(n)
+
+        @pl.loop(0, 4)
+        def _(i):
+            cols = columns_of(i, part)
+            p_buf[rows, cols] = mm(at_buf[rows, :], g_buf[:, cols], AB).astype(jnp.bfloat16)
+
+        for slot, block in enumerate((x_pair[0], x_far)):
+            remote(
+                p_buf.at[rows, columns_of(block, part)],
+                x1_buf.at[rows, pl.ds(slot * part, part)],
+                px_sem.at[0],
+                x1_sem.at[n],
+                x_dev[0],
+            ).start()
+
+    def landed(ref, sem):
+        remote(ref, ref, px_sem.at[0], sem, partner).wait_recv()
+
+    def x_second(n):
+        rows = group_rows(n)
+        landed(x1_buf.at[rows], x1_sem.at[n])
+        for slot, block in ((1, x_pair[1]), (0, x_at)):
+            cols = pl.ds(slot * part, part)
+            total = f32(p_buf[rows, columns_of(block, part)]) + f32(x1_buf[rows, cols])
+            x1_buf[rows, cols] = total.astype(jnp.bfloat16)
+            if slot == 1:
+                remote(
+                    x1_buf.at[rows, cols], x2_buf.at[rows], px_sem.at[1], x2_sem.at[n], x_dev[1]
+                ).start()
+
+    def y_first(n):
+        rows = group_rows(n)
+        landed(x2_buf.at[rows], x2_sem.at[n])
+        total = f32(x1_buf[rows, pl.ds(0, part)]) + f32(x2_buf[rows, :])
+        x2_buf[rows, :] = total.astype(jnp.bfloat16)
+        for slot, block in enumerate((y_pair[0], y_far)):
+            remote(
+                x2_buf.at[rows, columns_of(block, 128)],
+                y1_buf.at[rows, pl.ds(slot * 128, 128)],
+                px_sem.at[2],
+                y1_sem.at[n],
+                y_dev[0],
+            ).start()
+
+    def y_second(n):
+        rows = group_rows(n)
+        landed(y1_buf.at[rows], y1_sem.at[n])
+        for slot, block in ((1, y_pair[1]), (0, y_at)):
+            cols = pl.ds(slot * 128, 128)
+            total = f32(x2_buf[rows, columns_of(block, 128)]) + f32(y1_buf[rows, cols])
+            y1_buf[rows, cols] = total.astype(jnp.bfloat16)
+            if slot == 1:
+                remote(
+                    y1_buf.at[rows, cols], y2_buf.at[rows], px_sem.at[3], y2_sem.at[n], y_dev[1]
+                ).start()
+
+    def z_each(n, sent):
+        rows = group_rows(n)
+        owner = lax.div(n, groups // 2)
+        slot_rows = group_rows(lax.rem(n, groups // 2))
+        for b in range(2):
+            own = (zl == core) & (owner == core) & (zh == b)
+            copy = remote(
+                y2_buf.at[rows],
+                zr_buf.at[2 * zh + zl, slot_rows],
+                px_sem.at[4],
+                zr_sem.at[lax.rem(n, groups // 2)],
+                device(col, b, core, owner),
+            )
+
+            @pl.when(jnp.logical_not(own))
+            def _():
+                if sent:
+                    copy.wait_send()
+                else:
+                    copy.start()
+
+            if not sent:
+
+                @pl.when(own)
+                def _():
+                    zr_buf[2 * zh + zl, slot_rows, :] = y2_buf[rows, :]
+
+    def z_send(n):
+        rows = group_rows(n)
+        landed(y2_buf.at[rows], y2_sem.at[n])
+        total = f32(y1_buf[rows, pl.ds(0, 128)]) + f32(y2_buf[rows, :])
+        y2_buf[rows, :] = total.astype(jnp.bfloat16)
+        z_each(n, False)
+
+    stages = (product, x_second, y_first, y_second, z_send)
+
+    def reduce_step(t):
+        for late, stage in enumerate(stages):
+
+            @pl.when((t >= late) & (t - late < groups))
+            def _():
+                stage(t - late)
+
     @pl.loop(0, heads)
     def _(h):
         @pl.when(h + 1 < heads)
@@ -310,17 +459,46 @@
         def _():
             finish(h - 2)
 
-    @pl.loop(0, wg_ref.shape[1] // 256)
-    def _(n):
-        cols = pl.ds(pl.multiple_of(n * 256, 256), 256)
-        wg_ref[:, cols] = mm(at_buf[...], g_buf[:, cols], AB).astype(jnp.bfloat16)
-
-    finish(heads - 2)
-    finish(heads - 1)
+        @pl.when(lax.rem(h, 2) == 1)
+        def _():
+            reduce_step(lax.div(h, 2))
+
+    @pl.loop(groups, groups + len(stages) - 1)
+    def _(t):
+        @pl.when(t < groups + 2)
+        def _():
+            finish(t - groups + heads - 2)
+
+        reduce_step(t)
+
+    for n in range(groups // 2):
+        rows = pl.ds(n * group, group)
+        every = zr_buf.at[:, rows]
+        some = zr_buf.at[pl.ds(0, 3), rows]
+
+        @pl.when(zl == core)
+        def _():
+            landed(some, zr_sem.at[n])
+
+        @pl.when(zl != core)
+        def _():
+            landed(every, zr_sem.at[n])
+
+        total = f32(zr_buf[0, rows, :])
+        for i in range(1, 4):
+            total = total + f32(zr_buf[i, rows, :])
+        wg_ref[rows, :] = jnp.where(zh == 0, total[:, :64], total[:, 64:])
 
     for ref, slot in ((k_ref, 0), (v_ref, 1), (q_ref, 2)):
         remote(ref, ref, zs_sem.at[slot], o_sem.at[0], partner).wait_send()
-    remote(g_ref, g_ref, zs_sem.at[3], o_sem.at[0], partner).wait_send()
+    remote(gm_buf, gm_buf, zs_sem.at[3], o_sem.at[0], partner).wait_send()
+    for buf, slot in ((x1_buf, 0), (x2_buf, 1), (y1_buf, 2), (y2_buf, 3)):
+        remote(buf, buf, px_sem.at[slot], o_sem.at[0], partner).wait_send()
+
+    @pl.loop(0, groups)
+    def _(n):
+        z_each(n, True)
+
 
     @pl.when(core != zl)
     def _():
@@ -340,24 +518,28 @@
         remote(out, out, os_sem.at[slot], o_sem.at[slot], partner).wait_recv()
 
 
-def attention(queries, keys, values, grad_masked, proj_weight):
+def per_device(queries, keys, values, out_grad, proj_weight, lengths):
     tokens, width = queries.shape[1:]
     half = width // 2
     heads = half // HEAD_DIM
-    grad_width = grad_masked.shape[1]
+    grad_width = out_grad.shape[2]
+    groups = heads // 2
     any_space = pl.BlockSpec(memory_space=pl.ANY)
     dma = pltpu.SemaphoreType.DMA
     bf16 = jnp.bfloat16
 
-    def vmem(rows, cols, dtype=bf16):
-        return pltpu.VMEM((rows, cols), dtype)
+    def vmem(*shape, dtype=bf16):
+        return pltpu.VMEM(shape, dtype)
 
     pair = vmem(2 * tokens, half)
     outs = jax.ShapeDtypeStruct(queries.shape, bf16)
+    weight_grad = jax.ShapeDtypeStruct(
+        (width // lax.axis_size("dp"), grad_width // lax.axis_size("seq")), jnp.float32
+    )
     return pl.pallas_call(
         attention_kernel,
-        out_shape=(outs, outs, outs, jax.ShapeDtypeStruct((half, grad_width), bf16)),
-        in_specs=[any_space] * 5,
+        out_shape=(outs, outs, outs, weight_grad),
+        in_specs=[any_space] * 5 + [pl.BlockSpec(memory_space=pltpu.SMEM)],
         out_specs=(any_space, any_space, any_space, pl.BlockSpec(memory_space=pltpu.VMEM)),
         scratch_shapes=[
             pair,
@@ -372,10 +554,24 @@
             pair,
             pair,
             pair,
-            vmem(2 * tokens, half, jnp.float32),
-            vmem(2 * tokens, half, jnp.float32),
-            pair,
-            pair,
+            vmem(2 * tokens, half, dtype=jnp.float32),
+            vmem(2 * tokens, half, dtype=jnp.float32),
+            pair,
+            pair,
+            vmem(tokens, grad_width),
+            vmem(half, grad_width),
+            vmem(half, grad_width // 2),
+            vmem(half, grad_width // 4),
+            vmem(half, grad_width // 8),
+            vmem(half, grad_width // 16),
+            vmem(4, half // 2, grad_width // 16),
+            dma,
+            dma((5,)),
+            dma((groups,)),
+            dma((groups,)),
+            dma((groups,)),
+            dma((groups,)),
+            dma((groups // 2,)),
             dma((6,)),
             dma((heads,)),
             dma((heads,)),
@@ -397,33 +593,7 @@
             collective_id=0, has_side_effects=True, vmem_limit_bytes=66_000_000
         ),
         name="attention",
-    )(queries, keys, values, grad_masked, proj_weight)
-
-
-def reduce_weight(partial):
-    blocks = lax.axis_size("seq")
-    half, width = partial.shape
-    pieces = jnp.moveaxis(partial.reshape(half, blocks, width // blocks), 1, 0)
-    arrived = lax.all_to_all(pieces, "seq", split_axis=0, concat_axis=0, tiled=True)
-    summed = arrived.astype(jnp.float32).sum(axis=0)
-    core = lax.rem(lax.axis_index("dp"), 2)
-    rows = summed.reshape(2, half // 2, width // blocks)
-    none = jnp.zeros_like(rows)
-    padded = jnp.concatenate(
-        [jnp.where(core == 0, rows, none), jnp.where(core == 1, rows, none)], axis=0
-    )
-    parts = lax.all_to_all(padded, "dp", split_axis=0, concat_axis=0, tiled=True)
-    return parts.sum(axis=0)
-
-
-def per_device(queries, keys, values, out_grad, proj_weight, lengths):
-    tokens = queries.shape[1]
-    position = lax.axis_index("seq")
-    query_pos = position * tokens + jnp.arange(tokens, dtype=jnp.int32)
-    live = (query_pos < lengths[0]).astype(jnp.bfloat16)
-    grad_masked = out_grad[0] * live[:, None]
-    dq, dk, dv, partial = attention(queries, keys, values, grad_masked, proj_weight)
-    return dq, dk, dv, reduce_weight(partial)
+    )(queries, keys, values, out_grad, proj_weight, lengths)
 
 
 def solution(mesh):

time: 253 us -> 191 us (0.75)
  the two profiles are of different devices: /device:TPU:1 before, /device:TPU:19 now
where the time goes in v2:
time: 191 us
  Pallas kernels  182 us (95%)
  local copies, waits for them, and re-layouts  7.69 us (4%)
    pallas_call x1, Pallas kernels, per_device(): pl.pallas_call(attention_kernel, out_shape=(outs, outs, outs, weight_grad...  182 us
    unnamed x7, local copies, waits for them, and re-layouts  5.97 us

profile of v2, /device:TPU:19, one launch (start us, length us, event | category | flops | bytes accessed | tf_op | source)
XLA Modules:
  0.0 191.2 jit_solution(8513167514355405039)
XLA Ops:
  1.3 182.3 %attention.1 = (bf16[1,384,2048]{2,1,0:T(8,128)(2,1)}, bf16[1,384,2048]{2,1,0:T(8,128)(2,1)}, bf16[1,384,2048]{2,1,0:T(8,128)(2,1)}, f32[512,64]{1,0:T(8,128)}) custom-call(bf16[1,384,2048]{2,1,0:T(8,128)(2,1)} %q_ref.1, bf16[1,384,2048]{2,1,0:T(8,128)(2,1)} %k_ref.1, bf16[1,384,2048]{2,1,0:T(8,128)(2,1)} %v_ref.1, bf16[1,384,2048]{2,1,0:T(8,128)(2,1)} %g_ref.1, ...), custom_call_target="tpu_custom_call" | custom-call | tf_op jit(solution)/shard_map/attention/pallas_call | solution.py:539
  183.5 1.7 copy.10
  185.3 0.0 copy-start.1
  185.3 2.8 %copy.15 = bf16[1,384,2048]{2,1,0:T(8,128)(2,1)} copy(bf16[1,384,2048]{2,1,0:T(8,128)(2,1)} %get-tuple-element.12) | data formatting | bytes 3145728
  188.1 0.0 copy-done.1
  188.1 0.0 copy-start
  188.1 1.1 copy.16
  189.3 0.8 copy-done
  190.1 1.1 copy.17
Async XLA Ops:
  185.3 2.9 %copy-start.1 = (bf16[1,384,2048]{2,1,0:T(8,128)(2,1)S(1)}, bf16[1,384,2048]{2,1,0:T(8,128)(2,1)}, u32[]{:S(2)}) copy-start(bf16[1,384,2048]{2,1,0:T(8,128)(2,1)} %get-tuple-element.13) | copy-start | bytes 4718596
  188.1 2.0 %copy-start = (bf16[1,384,2048]{2,1,0:T(8,128)(2,1)S(1)}, bf16[1,384,2048]{2,1,0:T(8,128)(2,1)}, u32[]{:S(2)}) copy-start(bf16[1,384,2048]{2,1,0:T(8,128)(2,1)} %get-tuple-element.14) | copy-start | bytes 4718596

commit v3 on v1

--- a/solution.py
+++ b/solution.py
@@ -1,5 +1,3 @@
-import functools
-
 import jax
 import jax.numpy as jnp
 from jax import lax
@@ -9,6 +7,10 @@
 
 HEAD_DIM = 128
 LOG2E = 1.4426950408889634
+QUERY_LAG = 2
+KEY_LAG = 4
+AHEAD = 4
+SUM_LAG = 2
 MESH = pl.DeviceIdType.MESH
 
 AB = (((1,), (0,)), ((), ()))
@@ -25,6 +27,7 @@
     v_ref,
     g_ref,
     w_ref,
+    len_ref,
     dq_ref,
     dk_ref,
     dv_ref,
@@ -45,6 +48,17 @@
     vo_buf,
     kf_buf,
     vf_buf,
+    gm_buf,
+    p_buf,
+    r1_buf,
+    r2_buf,
+    zs_buf,
+    zr_buf,
+    gl_sem,
+    px_sem,
+    r1_sem,
+    r2_sem,
+    zr_sem,
     zs_sem,
     kz_sem,
     vz_sem,
@@ -52,6 +66,7 @@
     g_sem,
     gx_sem,
     w_sem,
+    wx_sem,
     wl_sem,
     ys_sem,
     ky_sem,
@@ -84,8 +99,20 @@
     previous = device(lax.rem(col + columns - 1, columns), zh, zl, core)
     partner = device(col, zh, zl, 1 - core)
 
+    g_local = pltpu.make_async_copy(g_ref.at[0], gm_buf, gl_sem)
+    g_local.start()
+
+    x_at = lax.div(col, 4)
+    y_at = lax.rem(col, 4)
+
+    def ring(at, step):
+        return lax.rem(at + step + 4, 4)
+
+    x_up, x_down = (device(4 * ring(x_at, i) + y_at, zh, zl, core) for i in (1, -1))
+    y_up, y_down = (device(4 * x_at + ring(y_at, i), zh, zl, core) for i in (1, -1))
+
     barrier = pltpu.get_barrier_semaphore()
-    greeted = [following, previous]
+    greeted = [following, previous, x_up, x_down, y_up, y_down]
     for i in range(1, 8):
         greeted.append(
             device(
@@ -97,7 +124,8 @@
         )
     for other in greeted:
         pl.semaphore_signal(barrier, inc=1, device_id=other, device_id_type=MESH)
-    pl.semaphore_wait(barrier, len(greeted))
+    with jax.named_scope("barrier"):
+        pl.semaphore_wait(barrier, len(greeted))
 
     def remote(src, dst, send_sem, recv_sem, to):
         return pltpu.make_async_remote_copy(
@@ -129,45 +157,101 @@
                 targets[t],
             ).start()
 
-    send_home(k_ref, k_buf, 2 * tokens, 0, kz_sem, 0)
-    send_home(v_ref, v_buf, 2 * tokens, 0, vz_sem, 1)
-    for t in range(2):
-        cols = pl.ds(t * half, half)
-        remote(
-            g_ref.at[:, cols],
-            g_buf.at[my_rows, cols],
-            zs_sem.at[3],
-            g_sem,
-            targets[t],
-        ).start()
+    far = core != zl
+    piece_rows = quarter // 8
     w_rows = pl.ds(pl.multiple_of(core * quarter, quarter), quarter)
     w_local = pltpu.make_async_copy(w_ref, w_buf.at[w_rows], wl_sem)
-
-    def w_send(to):
-        return remote(w_ref, w_buf.at[w_rows], zs_sem.at[4], w_sem, to)
-
-    w_far = [device(col, b, 1 - zl, zl) for b in range(2)]
-
-    @pl.when(core == zl)
+    w_swap = remote(w_ref, w_buf.at[w_rows], zs_sem.at[4], w_sem.at[2], partner)
+    w_axes = ((x_at, x_down), (y_at, y_down))
+
+    def w_piece(axis, j, at):
+        first_row = j * quarter + axis * (quarter // 2) + at * piece_rows
+        return w_buf.at[pl.ds(pl.multiple_of(first_row, piece_rows), piece_rows)]
+
+    def w_source(axis):
+        first_row = axis * (quarter // 2) + w_axes[axis][0] * piece_rows
+        return w_ref.at[pl.ds(pl.multiple_of(first_row, piece_rows), piece_rows)]
+
+    w_out = [
+        remote(
+            w_source(axis),
+            w_piece(axis, core, w_axes[axis][0]),
+            zs_sem.at[4],
+            w_sem.at[axis],
+            device(col, b, 1 - zl, zl),
+        )
+        for axis in range(2)
+        for b in range(2)
+    ]
+
+    def w_hop(axis, step):
+        at, down = w_axes[axis]
+        pieces = [w_piece(axis, j, ring(at, step)) for j in range(2)]
+        return [
+            remote(piece, piece, wx_sem.at[6], wx_sem.at[2 * step + axis], down)
+            for piece in pieces
+        ]
+
+    def w_wait(sem):
+        pieces = w_buf.at[pl.ds(0, 2 * piece_rows)]
+        with jax.named_scope("w_wait"):
+            remote(pieces, pieces, zs_sem.at[4], sem, partner).wait_recv()
+
+    def w_step(step):
+        @pl.when(far)
+        def _():
+            for axis in range(2):
+                w_wait(w_sem.at[axis] if step == 0 else wx_sem.at[2 * step - 2 + axis])
+                if step < 3:
+                    for copy in w_hop(axis, step):
+                        copy.start()
+
+    @pl.when(far)
+    def _():
+        w_swap.start()
+
+    @pl.when(jnp.logical_not(far))
     def _():
         w_local.start()
 
-    @pl.when(core != zl)
-    def _():
-        w_send(partner).start()
-
     @pl.when(zh == core)
     def _():
-        for to in w_far:
-            w_send(to).start()
-
-    send_home(q_ref, q_buf, 0, 0, qz_sem, 2)
-
-    @pl.loop(1, heads)
-    def _(h):
+        for copy in w_out:
+            copy.start()
+
+    def send_keys(h):
         send_home(k_ref, k_buf, 2 * tokens, h, kz_sem, 0)
         send_home(v_ref, v_buf, 2 * tokens, h, vz_sem, 1)
+
+    def send_queries(h):
         send_home(q_ref, q_buf, 0, h, qz_sem, 2)
+
+    g_parts = 4
+    g_width = half // g_parts
+    send_keys(0)
+    g_local.wait()
+    limit = len_ref[0] - seq * tokens
+    live = lax.broadcasted_iota(jnp.int32, gm_buf.shape, 0) < limit
+    gm_buf[...] = jnp.where(live, gm_buf[...], jnp.zeros_like(gm_buf))
+    for i in range(g_parts):
+        for t in range(2):
+            cols = pl.ds(t * half + i * g_width, g_width)
+            remote(
+                gm_buf.at[:, cols], g_buf.at[my_rows, cols], zs_sem.at[3], g_sem.at[i], targets[t]
+            ).start()
+        if i + 1 < g_parts:
+            send_keys(i + 1)
+    send_queries(0)
+
+    @pl.loop(g_parts, heads)
+    def _(h):
+        send_keys(h)
+        for i in range(2):
+            n = 2 * (h - g_parts) + 1 + i
+
+            @pl.when(n < heads)
+            def _():
+                send_queries(n)
 
     def forward(h):
         for buf, got, sem, slot in (
@@ -175,31 +259,50 @@
             (v_buf, vz_sem, vy_sem, 1),
         ):
             own = buf.at[own_rows, lanes(h)]
-            remote(own, own, zs_sem.at[0], got.at[h], partner).wait_recv()
+            with jax.named_scope("kv_wait"):
+                remote(own, own, zs_sem.at[0], got.at[h], partner).wait_recv()
             remote(own, buf.at[halo_rows, lanes(h)], ys_sem.at[slot], sem.at[h], following).start()
 
+    def g_piece(i):
+        cols = pl.ds(pl.multiple_of(core * half + i * g_width, g_width), g_width)
+        return g_buf.at[:, cols]
+
+    def g_swap(i):
+        return remote(g_piece(i), g_piece(i), zs_sem.at[5], gx_sem.at[i], partner)
+
+    def g_exchange(i):
+        with jax.named_scope("g_wait"):
+            remote(g_piece(i), g_piece(i), zs_sem.at[3], g_sem.at[i], partner).wait_recv()
+        g_swap(i).start()
+
+    w_step(0)
     forward(0)
-
-    g_half = g_buf.at[:, my_half]
-    remote(g_half, g_half, zs_sem.at[3], g_sem, partner).wait_recv()
-    g_swap = remote(g_half, g_half, zs_sem.at[5], gx_sem, partner)
-    g_swap.start()
-
-    @pl.when(core == zl)
+    w_step(1)
+    g_exchange(0)
+    forward(1)
+    w_step(2)
+    g_exchange(1)
+    w_step(3)
+    forward(2)
+    g_exchange(2)
+    forward(3)
+    g_exchange(3)
+
+    @pl.when(jnp.logical_not(far))
     def _():
         w_local.wait()
-        w_send(partner).wait_recv()
-
-    @pl.when(core != zl)
-    def _():
-        remote(w_buf, w_buf, zs_sem.at[4], w_sem, partner).wait_recv()
-
-    g_swap.wait_recv()
-
-    @pl.loop(0, 2 * tokens // 256)
-    def _(n):
-        rows = pl.ds(pl.multiple_of(n * 256, 256), 256)
-        do_buf[:, rows] = mm(w_buf[...], g_buf[rows, :], ABT).astype(jnp.bfloat16)
+        remote(w_ref, w_ref, zs_sem.at[4], w_sem.at[2], partner).wait_recv()
+
+    with jax.named_scope("gx_wait"):
+        for i in range(g_parts):
+            g_swap(i).wait_recv()
+
+    with jax.named_scope("out_bwd"):
+
+        @pl.loop(0, 2 * tokens // 256)
+        def _(n):
+            rows = pl.ds(pl.multiple_of(n * 256, 256), 256)
+            do_buf[:, rows] = mm(w_buf[...], g_buf[rows, :], ABT).astype(jnp.bfloat16)
 
     first = jnp.where(col == 0, -1e30, 0.0).astype(jnp.float32)
     key_pos = lax.broadcasted_iota(jnp.int32, (tokens, tokens), 0)
@@ -283,81 +386,251 @@
             (vr_buf, vo_buf, vf_buf, dv_ref, vr_sem, 2),
         ):
             piece = got.at[:, at]
-            remote(piece, piece, rs_sem.at[0], sem.at[h], partner).wait_recv()
+            with jax.named_scope("back_wait"):
+                remote(piece, piece, rs_sem.at[0], sem.at[h], partner).wait_recv()
             done[:, at] = (own[:, at] + got[:, at].astype(jnp.float32)).astype(jnp.bfloat16)
             send_out(done, out, slot, h)
 
+    def give_back(t):
+        for lag, task in ((QUERY_LAG, lambda h: send_out(dq_buf, dq_ref, 0, h)), (KEY_LAG, finish)):
+
+            @pl.when((t >= lag) & (t - lag < heads))
+            def _():
+                task(t - lag)
+
+    group = 2 * HEAD_DIM
+    groups = half // group
+    wide = 128
+    part = 4 * wide
+    along_x = core == 0
+    outer_at = jnp.where(along_x, x_at, y_at)
+    inner_at = jnp.where(along_x, y_at, x_at)
+
+    def device_of(first, second):
+        return tuple(jnp.where(along_x, a, b) for a, b in zip(first, second))
+
+    outer_up = device_of(x_up, y_up)
+    inner_up = device_of(y_up, x_up)
+
+    def group_rows(n):
+        return pl.ds(pl.multiple_of(n * group, group), group)
+
+    def columns_of(n, size):
+        return pl.ds(pl.multiple_of(n * size, size), size)
+
+    def f32(value):
+        return value.astype(jnp.float32)
+
+    def landed(ref, sem):
+        with jax.named_scope("sum_wait"):
+            remote(ref, ref, px_sem.at[0], sem, partner).wait_recv()
+
+    def outer_send(n, step, src):
+        remote(
+            src, r1_buf.at[step, group_rows(n)], px_sem.at[step], r1_sem.at[step, n], outer_up
+        ).start()
+
+    def inner_send(n, step, src):
+        remote(
+            src, r2_buf.at[step, group_rows(n)], px_sem.at[3 + step], r2_sem.at[step, n], inner_up
+        ).start()
+
+    def product(n):
+        rows = group_rows(n)
+
+        @pl.loop(0, 4)
+        def _(x):
+            term = mm(at_buf[rows, :], g_buf[:, columns_of(x, part)], AB).astype(jnp.bfloat16)
+            for y in range(4):
+                place = jnp.where(along_x, 4 * x + y, 4 * y + x)
+                p_buf[rows, columns_of(place, wide)] = term[:, y * wide : (y + 1) * wide]
+
+        outer_send(n, 0, p_buf.at[rows, columns_of(ring(outer_at, -1), part)])
+
+    def outer(step, n):
+        rows = group_rows(n)
+        landed(r1_buf.at[step, rows], r1_sem.at[step, n])
+        cols = columns_of(ring(outer_at, -2 - step), part)
+        total = f32(p_buf[rows, cols]) + f32(r1_buf[step, rows, :])
+        r1_buf[step, rows, :] = total.astype(jnp.bfloat16)
+        if step < 2:
+            outer_send(n, step + 1, r1_buf.at[step, rows])
+        else:
+            inner_send(n, 0, r1_buf.at[2, rows, columns_of(ring(inner_at, -1), wide)])
+
+    def inner(step, n):
+        rows = group_rows(n)
+        landed(r2_buf.at[step, rows], r2_sem.at[step, n])
+        cols = columns_of(ring(inner_at, -2 - step), wide)
+        total = f32(r1_buf[2, rows, cols]) + f32(r2_buf[step, rows, :])
+        if step < 2:
+            r2_buf[step, rows, :] = total.astype(jnp.bfloat16)
+            inner_send(n, step + 1, r2_buf.at[step, rows])
+        else:
+            z_send(n, total)
+
+    short = group // 2
+
+    def packed_rows(n):
+        return pl.ds(pl.multiple_of(n * short, short), short)
+
+    def z_each(n, sent):
+        owner = lax.div(n, groups // 2)
+        slot_rows = packed_rows(lax.rem(n, groups // 2))
+        for b in range(2):
+            own = (zl == core) & (owner == core) & (zh == b)
+            copy = remote(
+                zs_buf.at[b, packed_rows(n)],
+                zr_buf.at[2 * zh + zl, slot_rows],
+                px_sem.at[6],
+                zr_sem.at[lax.rem(n, groups // 2)],
+                device(col, b, core, owner),
+            )
+
+            @pl.when(jnp.logical_not(own))
+            def _():
+                if sent:
+                    copy.wait_send()
+                else:
+                    copy.start()
+
+            if not sent:
+
+                @pl.when(own)
+                def _():
+                    zr_buf[2 * zh + zl, slot_rows, :] = zs_buf[b, packed_rows(n), :]
+
+    def z_send(n, total):
+        upper, lower = total[:short], total[short:]
+        left = lax.broadcasted_iota(jnp.int32, upper.shape, 1) < wide // 2
+        for b, packed in enumerate(
+            (
+                jnp.where(left, upper, pltpu.roll(lower, wide // 2, 1)),
+                jnp.where(left, pltpu.roll(upper, wide // 2, 1), lower),
+            )
+        ):
+            zs_buf[b, packed_rows(n), :] = packed.astype(jnp.bfloat16)
+        z_each(n, False)
+
+    stages = [product]
+    stages += [lambda n, step=step: outer(step, n) for step in range(3)]
+    stages += [lambda n, step=step: inner(step, n) for step in range(3)]
+
+    def reduce_step(t):
+        for late, stage in enumerate(stages):
+            n = t - 1 - late - (SUM_LAG if late else 0)
+
+            @pl.when((n >= 0) & (lax.rem(n + 2 * heads, 2) == 0) & (n < 2 * groups))
+            def _():
+                with jax.named_scope(f"stage{late}"):
+                    stage(lax.div(n, 2))
+
     @pl.loop(0, heads)
     def _(h):
-        @pl.when(h + 1 < heads)
+        @pl.when(h + AHEAD < heads)
         def _():
-            forward(h + 1)
+            forward(h + AHEAD)
 
         at = lanes(h)
         piece = q_buf.at[:, at]
-        remote(piece, piece, zs_sem.at[2], qz_sem.at[h], partner).wait_recv()
+        with jax.named_scope("q_wait"):
+            remote(piece, piece, zs_sem.at[2], qz_sem.at[h], partner).wait_recv()
         for buf, sem in ((k_buf, ky_sem), (v_buf, vy_sem)):
             piece = buf.at[halo_rows, at]
-            remote(piece, piece, ys_sem.at[0], sem.at[h], partner).wait_recv()
-        head(h)
+            with jax.named_scope("halo_wait"):
+                remote(piece, piece, ys_sem.at[0], sem.at[h], partner).wait_recv()
+        with jax.named_scope("head"):
+            head(h)
         for src, dst, sem, slot in ((kh_buf, kr_buf, kr_sem, 0), (vh_buf, vr_buf, vr_sem, 1)):
             remote(
                 src.at[:, at], dst.at[:, at], rs_sem.at[slot], sem.at[h], previous
             ).start()
-        send_out(dq_buf, dq_ref, 0, h)
-
-        @pl.when(h >= 2)
+        give_back(h)
+
+        reduce_step(h)
+
+    @pl.loop(heads, heads + len(stages) + SUM_LAG)
+    def _(t):
+        give_back(t)
+        reduce_step(t)
+
+    for n in range(groups // 2):
+        rows = pl.ds(n * short, short)
+        every = zr_buf.at[:, rows]
+        some = zr_buf.at[pl.ds(0, 3), rows]
+
+        @pl.when(zl == core)
         def _():
-            finish(h - 2)
-
-    @pl.loop(0, wg_ref.shape[1] // 256)
-    def _(n):
-        cols = pl.ds(pl.multiple_of(n * 256, 256), 256)
-        wg_ref[:, cols] = mm(at_buf[...], g_buf[:, cols], AB).astype(jnp.bfloat16)
-
-    finish(heads - 2)
-    finish(heads - 1)
-
-    for ref, slot in ((k_ref, 0), (v_ref, 1), (q_ref, 2)):
-        remote(ref, ref, zs_sem.at[slot], o_sem.at[0], partner).wait_send()
-    remote(g_ref, g_ref, zs_sem.at[3], o_sem.at[0], partner).wait_send()
-
-    @pl.when(core != zl)
-    def _():
-        w_send(partner).wait_send()
-
-    @pl.when(zh == core)
-    def _():
-        for to in w_far:
-            w_send(to).wait_send()
-
-    g_swap.wait_send()
-    for buf, slot in ((kr_buf, 0), (vr_buf, 1)):
-        remote(buf, buf, ys_sem.at[slot], o_sem.at[0], partner).wait_send()
-        remote(buf, buf, rs_sem.at[slot], o_sem.at[0], partner).wait_send()
-    for buf, out, slot in ((dq_buf, dq_ref, 0), (kf_buf, dk_ref, 1), (vf_buf, dv_ref, 2)):
-        remote(buf, buf, os_sem.at[slot], o_sem.at[0], partner).wait_send()
-        remote(out, out, os_sem.at[slot], o_sem.at[slot], partner).wait_recv()
-
-
-def attention(queries, keys, values, grad_masked, proj_weight):
+            landed(some, zr_sem.at[n])
+
+        @pl.when(zl != core)
+        def _():
+            landed(every, zr_sem.at[n])
+
+        total = f32(zr_buf[0, rows, :])
+        for i in range(1, 4):
+            total = total + f32(zr_buf[i, rows, :])
+        wg_ref[pl.ds(n * group, short), :] = total[:, : wide // 2]
+        wg_ref[pl.ds(n * group + short, short), :] = total[:, wide // 2 :]
+
+    with jax.named_scope("drain"):
+        for ref, slot in ((k_ref, 0), (v_ref, 1), (q_ref, 2)):
+            remote(ref, ref, zs_sem.at[slot], o_sem.at[0], partner).wait_send()
+        remote(gm_buf, gm_buf, zs_sem.at[3], o_sem.at[0], partner).wait_send()
+        for step in range(3):
+            for buf, slot in ((r1_buf, step), (r2_buf, 3 + step)):
+                remote(buf.at[0], buf.at[0], px_sem.at[slot], o_sem.at[0], partner).wait_send()
+
+        @pl.loop(0, groups)
+        def _(n):
+            z_each(n, True)
+
+
+        @pl.when(far)
+        def _():
+            w_swap.wait_send()
+            for axis in range(2):
+                for step in range(3):
+                    for copy in w_hop(axis, step):
+                        copy.wait_send()
+
+        @pl.when(zh == core)
+        def _():
+            for copy in w_out:
+                copy.wait_send()
+
+        for i in range(g_parts):
+            g_swap(i).wait_send()
+        for buf, slot in ((kr_buf, 0), (vr_buf, 1)):
+            remote(buf, buf, ys_sem.at[slot], o_sem.at[0], partner).wait_send()
+            remote(buf, buf, rs_sem.at[slot], o_sem.at[0], partner).wait_send()
+        for buf, out, slot in ((dq_buf, dq_ref, 0), (kf_buf, dk_ref, 1), (vf_buf, dv_ref, 2)):
+            remote(buf, buf, os_sem.at[slot], o_sem.at[0], partner).wait_send()
+            remote(out, out, os_sem.at[slot], o_sem.at[slot], partner).wait_recv()
+
+
+def per_device(queries, keys, values, out_grad, proj_weight, lengths):
     tokens, width = queries.shape[1:]
     half = width // 2
     heads = half // HEAD_DIM
-    grad_width = grad_masked.shape[1]
+    grad_width = out_grad.shape[2]
+    groups = heads // 2
     any_space = pl.BlockSpec(memory_space=pl.ANY)
     dma = pltpu.SemaphoreType.DMA
     bf16 = jnp.bfloat16
 
-    def vmem(rows, cols, dtype=bf16):
-        return pltpu.VMEM((rows, cols), dtype)
+    def vmem(*shape, dtype=bf16):
+        return pltpu.VMEM(shape, dtype)
 
     pair = vmem(2 * tokens, half)
     outs = jax.ShapeDtypeStruct(queries.shape, bf16)
+    weight_grad = jax.ShapeDtypeStruct(
+        (width // lax.axis_size("dp"), grad_width // lax.axis_size("seq")), jnp.float32
+    )
     return pl.pallas_call(
         attention_kernel,
-        out_shape=(outs, outs, outs, jax.ShapeDtypeStruct((half, grad_width), bf16)),
-        in_specs=[any_space] * 5,
+        out_shape=(outs, outs, outs, weight_grad),
+        in_specs=[any_space] * 5 + [pl.BlockSpec(memory_space=pltpu.SMEM)],
         out_specs=(any_space, any_space, any_space, pl.BlockSpec(memory_space=pltpu.VMEM)),
         scratch_shapes=[
             pair,
@@ -372,17 +645,29 @@
             pair,
             pair,
             pair,
-            vmem(2 * tokens, half, jnp.float32),
-            vmem(2 * tokens, half, jnp.float32),
+            vmem(2 * tokens, half, dtype=jnp.float32),
+            vmem(2 * tokens, half, dtype=jnp.float32),
             pair,
             pair,
+            vmem(tokens, grad_width),
+            vmem(half, grad_width),
+            vmem(3, half, grad_width // 4),
+            vmem(3, half, grad_width // 16),
+            vmem(2, half // 2, grad_width // 16),
+            vmem(4, half // 4, grad_width // 16),
+            dma,
+            dma((7,)),
+            dma((3, groups)),
+            dma((3, groups)),
+            dma((groups // 2,)),
             dma((6,)),
             dma((heads,)),
             dma((heads,)),
             dma((heads,)),
-            dma,
-            dma,
-            dma,
+            dma((4,)),
+            dma((4,)),
+            dma((3,)),
+            dma((7,)),
             dma,
             dma((2,)),
             dma((heads,)),
@@ -397,33 +682,7 @@
             collective_id=0, has_side_effects=True, vmem_limit_bytes=66_000_000
         ),
         name="attention",
-    )(queries, keys, values, grad_masked, proj_weight)
-
-
-def reduce_weight(partial):
-    blocks = lax.axis_size("seq")
-    half, width = partial.shape
-    pieces = jnp.moveaxis(partial.reshape(half, blocks, width // blocks), 1, 0)
-    arrived = lax.all_to_all(pieces, "seq", split_axis=0, concat_axis=0, tiled=True)
-    summed = arrived.astype(jnp.float32).sum(axis=0)
-    core = lax.rem(lax.axis_index("dp"), 2)
-    rows = summed.reshape(2, half // 2, width // blocks)
-    none = jnp.zeros_like(rows)
-    padded = jnp.concatenate(
-        [jnp.where(core == 0, rows, none), jnp.where(core == 1, rows, none)], axis=0
-    )
-    parts = lax.all_to_all(padded, "dp", split_axis=0, concat_axis=0, tiled=True)
-    return parts.sum(axis=0)
-
-
-def per_device(queries, keys, values, out_grad, proj_weight, lengths):
-    tokens = queries.shape[1]
-    position = lax.axis_index("seq")
-    query_pos = position * tokens + jnp.arange(tokens, dtype=jnp.int32)
-    live = (query_pos < lengths[0]).astype(jnp.bfloat16)
-    grad_masked = out_grad[0] * live[:, None]
-    dq, dk, dv, partial = attention(queries, keys, values, grad_masked, proj_weight)
-    return dq, dk, dv, reduce_weight(partial)
+    )(queries, keys, values, out_grad, proj_weight, lengths)
 
 
 def solution(mesh):

time: 253 us -> 165 us (0.65)
  the two profiles are of different devices: /device:TPU:1 before, /device:TPU:19 now
where the time goes in v3:
time: 165 us; the launch traced here: 163 us
  Pallas kernels  154 us (93%)
  local copies, waits for them, and re-layouts  7.69 us (5%)
    pallas_call x1, Pallas kernels, per_device(): pl.pallas_call(attention_kernel, out_shape=(outs, outs, outs, weight_grad...  154 us
    unnamed x7, local copies, waits for them, and re-layouts  5.97 us

profile of v3, /device:TPU:19, one launch (start us, length us, event | category | flops | bytes accessed | tf_op | source)
XLA Modules:
  0.0 163.2 jit_solution(13924588531238214840)
XLA Ops:
  1.3 154.2 %attention.1 = (bf16[1,384,2048]{2,1,0:T(8,128)(2,1)}, bf16[1,384,2048]{2,1,0:T(8,128)(2,1)}, bf16[1,384,2048]{2,1,0:T(8,128)(2,1)}, f32[512,64]{1,0:T(8,128)}) custom-call(bf16[1,384,2048]{2,1,0:T(8,128)(2,1)} %q_ref.1, bf16[1,384,2048]{2,1,0:T(8,128)(2,1)} %k_ref.1, bf16[1,384,2048]{2,1,0:T(8,128)(2,1)} %v_ref.1, bf16[1,384,2048]{2,1,0:T(8,128)(2,1)} %g_ref.1, ...), custom_call_target="tpu_custom_call" | custom-call | tf_op jit(solution)/shard_map/attention/pallas_call | solution.py:630
  155.5 1.7 %copy.10 = f32[512,64]{0,1:T(8,128)} copy(f32[512,64]{1,0:T(8,128)} %get-tuple-element.7) | data formatting | bytes 262144 | tf_op jit(solution)/shard_map/attention/pallas_call | solution.py:630
  157.2 0.0 copy-start.1
  157.2 2.8 %copy.15 = bf16[1,384,2048]{2,1,0:T(8,128)(2,1)} copy(bf16[1,384,2048]{2,1,0:T(8,128)(2,1)} %get-tuple-element.12) | data formatting | bytes 3145728
  160.1 0.0 copy-done.1
  160.1 0.0 copy-start
  160.1 1.1 copy.16
  161.2 0.8 copy-done
  162.1 1.1 copy.17
Async XLA Ops:
  157.2 2.9 %copy-start.1 = (bf16[1,384,2048]{2,1,0:T(8,128)(2,1)S(1)}, bf16[1,384,2048]{2,1,0:T(8,128)(2,1)}, u32[]{:S(2)}) copy-start(bf16[1,384,2048]{2,1,0:T(8,128)(2,1)} %get-tuple-element.13) | copy-start | bytes 4718596
  160.1 2.0 %copy-start = (bf16[1,384,2048]{2,1,0:T(8,128)(2,1)S(1)}, bf16[1,384,2048]{2,1,0:T(8,128)(2,1)}, u32[]{:S(2)}) copy-start(bf16[1,384,2048]{2,1,0:T(8,128)(2,1)} %get-tuple-element.14) | copy-start | bytes 4718596

commit v4 on v3

--- a/solution.py
+++ b/solution.py
@@ -1,3 +1,5 @@
+import functools
+
 import jax
 import jax.numpy as jnp
 from jax import lax
@@ -10,7 +12,9 @@
 QUERY_LAG = 2
 KEY_LAG = 4
 AHEAD = 4
-SUM_LAG = 2
+COPY_ROWS = 96
+PRODUCTS = (1, 3, 5, 7)
+SUMS = (3, 5, 6, 7)
 MESH = pl.DeviceIdType.MESH
 
 AB = (((1,), (0,)), ((), ()))
@@ -518,12 +522,14 @@
 
     def reduce_step(t):
         for late, stage in enumerate(stages):
-            n = t - 1 - late - (SUM_LAG if late else 0)
-
-            @pl.when((n >= 0) & (lax.rem(n + 2 * heads, 2) == 0) & (n < 2 * groups))
+            times = SUMS if late else PRODUCTS
+            due = functools.reduce(jnp.logical_or, [t - late == time for time in times])
+            n = sum((t - late > time).astype(jnp.int32) for time in times)
+
+            @pl.when(due)
             def _():
                 with jax.named_scope(f"stage{late}"):
-                    stage(lax.div(n, 2))
+                    stage(n)
 
     @pl.loop(0, heads)
     def _(h):
@@ -549,7 +555,7 @@
 
         reduce_step(h)
 
-    @pl.loop(heads, heads + len(stages) + SUM_LAG)
+    @pl.loop(heads, heads + max(KEY_LAG, SUMS[-1] + len(stages) - heads))
     def _(t):
         give_back(t)
         reduce_step(t)
@@ -570,8 +576,9 @@
         total = f32(zr_buf[0, rows, :])
         for i in range(1, 4):
             total = total + f32(zr_buf[i, rows, :])
-        wg_ref[pl.ds(n * group, short), :] = total[:, : wide // 2]
-        wg_ref[pl.ds(n * group + short, short), :] = total[:, wide // 2 :]
+        turned = total.T
+        wg_ref[:, pl.ds(n * group, short)] = turned[: wide // 2]
+        wg_ref[:, pl.ds(n * group + short, short)] = turned[wide // 2 :]
 
     with jax.named_scope("drain"):
         for ref, slot in ((k_ref, 0), (v_ref, 1), (q_ref, 2)):
@@ -607,6 +614,28 @@
         for buf, out, slot in ((dq_buf, dq_ref, 0), (kf_buf, dk_ref, 1), (vf_buf, dv_ref, 2)):
             remote(buf, buf, os_sem.at[slot], o_sem.at[0], partner).wait_send()
             remote(out, out, os_sem.at[slot], o_sem.at[slot], partner).wait_recv()
+
+
+def copy_kernel(a_ref, b_ref, c_ref, w_ref, a_out, b_out, c_out, w_out, held, in_sem, out_sem):
+    moves = []
+    for i, (src, dst) in enumerate(((a_ref, a_out), (b_ref, b_out), (c_ref, c_out))):
+        for n in range(src.shape[1] // COPY_ROWS):
+            rows = pl.ds(n * COPY_ROWS, COPY_ROWS)
+            room = held.at[i, rows]
+            moves.append(
+                (
+                    pltpu.make_async_copy(src.at[0, rows], room, in_sem.at[i, n]),
+                    pltpu.make_async_copy(room, dst.at[0, rows], out_sem.at[i, n]),
+                )
+            )
+    for move in moves:
+        move[0].start()
+    w_out[...] = w_ref[...]
+    for move in moves:
+        move[0].wait()
+        move[1].start()
+    for move in moves:
+        move[1].wait()
 
 
 def per_device(queries, keys, values, out_grad, proj_weight, lengths):
@@ -625,9 +654,9 @@
     pair = vmem(2 * tokens, half)
     outs = jax.ShapeDtypeStruct(queries.shape, bf16)
     weight_grad = jax.ShapeDtypeStruct(
-        (width // lax.axis_size("dp"), grad_width // lax.axis_size("seq")), jnp.float32
+        (grad_width // lax.axis_size("seq"), width // lax.axis_size("dp")), jnp.float32
     )
-    return pl.pallas_call(
+    results = pl.pallas_call(
         attention_kernel,
         out_shape=(outs, outs, outs, weight_grad),
         in_specs=[any_space] * 5 + [pl.BlockSpec(memory_space=pltpu.SMEM)],
@@ -683,6 +712,20 @@
         ),
         name="attention",
     )(queries, keys, values, out_grad, proj_weight, lengths)
+    pieces = tokens // COPY_ROWS
+    dq, dk, dv, turned = pl.pallas_call(
+        copy_kernel,
+        out_shape=(outs, outs, outs, weight_grad),
+        in_specs=[any_space] * 3 + [pl.BlockSpec(memory_space=pltpu.VMEM)],
+        out_specs=(any_space, any_space, any_space, pl.BlockSpec(memory_space=pltpu.VMEM)),
+        scratch_shapes=[vmem(3, tokens, width), dma((3, pieces)), dma((3, pieces))],
+        compiler_params=pltpu.CompilerParams(vmem_limit_bytes=66_000_000),
+        cost_estimate=pl.CostEstimate(
+            flops=0, bytes_accessed=12 * tokens * width, transcendentals=0
+        ),
+        name="results",
+    )(*results)
+    return dq, dk, dv, turned.T
 
 
 def solution(mesh):

time: 165 us -> 157 us (0.952); the launches traced: 163 us -> 157 us
  local copies, waits for them, and re-layouts: 7.69 us -> 0 us
  Pallas kernels: 154 us -> 156 us
    unnamed x7 -> x0, local copies, waits for them, and re-layouts: 5.97 us -> none
    pallas_call x0 -> x1, Pallas kernels: none -> 5.83 us  [per_device(): pl.pallas_call(copy_kernel, out_shape=(outs, outs, outs, weight_grad), in...]
    pallas_call x1, Pallas kernels: 154 us -> 150 us  [per_device(): pl.pallas_call(attention_kernel, out_shape=(outs, outs, outs, weight_grad...]
    pallas_call x1 -> x0, local copies, waits for them, and re-layouts: 1.72 us -> none  [per_device(): pl.pallas_call(attention_kernel, out_shape=(outs, outs, outs, weight_grad...]
where the time goes in v4:
time: 157 us
  Pallas kernels  156 us (99%)
    pallas_call x1, Pallas kernels, per_device(): pl.pallas_call(attention_kernel, out_shape=(outs, outs, outs, weight_grad...  150 us
    pallas_call x1, Pallas kernels, per_device(): pl.pallas_call(copy_kernel, out_shape=(outs, outs, outs, weight_grad), in...  5.83 us

profile of v4, /device:TPU:19, one launch (start us, length us, event | category | flops | bytes accessed | tf_op | source)
XLA Modules:
  0.0 157.0 jit_solution(8876618475166627876)
XLA Ops:
  1.3 149.9 %attention.1 = (bf16[1,384,2048]{2,1,0:T(8,128)(2,1)}, bf16[1,384,2048]{2,1,0:T(8,128)(2,1)}, bf16[1,384,2048]{2,1,0:T(8,128)(2,1)}, f32[64,512]{1,0:T(8,128)}) custom-call(bf16[1,384,2048]{2,1,0:T(8,128)(2,1)} %q_ref.1, bf16[1,384,2048]{2,1,0:T(8,128)(2,1)} %k_ref.1, bf16[1,384,2048]{2,1,0:T(8,128)(2,1)} %v_ref.1, bf16[1,384,2048]{2,1,0:T(8,128)(2,1)} %g_ref.1, ...), custom_call_target="tpu_custom_call" | custom-call | tf_op jit(solution)/shard_map/attention/pallas_call | solution.py:659
  151.2 5.8 %results.1 = (bf16[1,384,2048]{2,1,0:T(8,128)(2,1)}, bf16[1,384,2048]{2,1,0:T(8,128)(2,1)}, bf16[1,384,2048]{2,1,0:T(8,128)(2,1)}, f32[64,512]{1,0:T(8,128)}) custom-call(bf16[1,384,2048]{2,1,0:T(8,128)(2,1)} %get-tuple-element.12.a_ref, bf16[1,384,2048]{2,1,0:T(8,128)(2,1)} %get-tuple-element.13.b_ref, bf16[1,384,2048]{2,1,0:T(8,128)(2,1)} %get-tuple-element.14.c_ref, ...), custom_call_target="tpu_custom_call" | custom-call | bytes 9437184 | tf_op jit(solution)/shard_map/results/pallas_call | solution.py:716

commit v5 on v4

--- a/solution.py
+++ b/solution.py
@@ -11,10 +11,10 @@
 LOG2E = 1.4426950408889634
 QUERY_LAG = 2
 KEY_LAG = 4
-AHEAD = 4
-COPY_ROWS = 96
+AHEAD = 3
+COPY_ROWS = 192
 PRODUCTS = (1, 3, 5, 7)
-SUMS = (3, 5, 6, 7)
+SUMS = (4, 5, 6, 7)
 MESH = pl.DeviceIdType.MESH
 
 AB = (((1,), (0,)), ((), ()))
@@ -533,7 +533,7 @@
 
     @pl.loop(0, heads)
     def _(h):
-        @pl.when(h + AHEAD < heads)
+        @pl.when((h >= 1) & (h + AHEAD < heads))
         def _():
             forward(h + AHEAD)
 

time: 157 us -> 156 us (level)
  no operation moved by 1% of the time
where the time goes in v5:
time: 156 us
  Pallas kernels  155 us (99%)
    pallas_call x1, Pallas kernels, per_device(): pl.pallas_call(attention_kernel, out_shape=(outs, outs, outs, weight_grad...  149 us
    pallas_call x1, Pallas kernels, per_device(): pl.pallas_call(copy_kernel, out_shape=(outs, outs, outs, weight_grad), in...  5.52 us

profile of v5, /device:TPU:19, one launch (start us, length us, event | category | flops | bytes accessed | tf_op | source)
XLA Modules:
  0.0 156.1 jit_solution(43440169074713758)
XLA Ops:
  1.3 149.3 %attention.1 = (bf16[1,384,2048]{2,1,0:T(8,128)(2,1)}, bf16[1,384,2048]{2,1,0:T(8,128)(2,1)}, bf16[1,384,2048]{2,1,0:T(8,128)(2,1)}, f32[64,512]{1,0:T(8,128)}) custom-call(bf16[1,384,2048]{2,1,0:T(8,128)(2,1)} %q_ref.1, bf16[1,384,2048]{2,1,0:T(8,128)(2,1)} %k_ref.1, bf16[1,384,2048]{2,1,0:T(8,128)(2,1)} %v_ref.1, bf16[1,384,2048]{2,1,0:T(8,128)(2,1)} %g_ref.1, ...), custom_call_target="tpu_custom_call" | custom-call | tf_op jit(solution)/shard_map/attention/pallas_call | solution.py:659
  150.6 5.5 %results.1 = (bf16[1,384,2048]{2,1,0:T(8,128)(2,1)}, bf16[1,384,2048]{2,1,0:T(8,128)(2,1)}, bf16[1,384,2048]{2,1,0:T(8,128)(2,1)}, f32[64,512]{1,0:T(8,128)}) custom-call(bf16[1,384,2048]{2,1,0:T(8,128)(2,1)} %get-tuple-element.12.a_ref, bf16[1,384,2048]{2,1,0:T(8,128)(2,1)} %get-tuple-element.13.b_ref, bf16[1,384,2048]{2,1,0:T(8,128)(2,1)} %get-tuple-element.14.c_ref, ...), custom_call_target="tpu_custom_call" | custom-call | bytes 9437184 | tf_op jit(solution)/shard_map/results/pallas_call | solution.py:716
